TPU v7x, 128 devices: a whole 4x4x4 slice. The times are simulated.
128 devices in a mesh: dp: 1, tx: 16 (over z, y), ty: 8 (over x, core).
Axes of the slice: x: 4, y: 4, z: 4, core: 2. Of those that a mesh axis runs over, the one named last changes fastest.
Arguments:
- residual: float32 [1024, 2048], P('dp', 'tx')
- norm_w: float32 [2, 2048], P(None, 'tx')
- w_in: bfloat16 [2, 2048, 2, 4096], P(None, 'tx', None, 'ty')
- conv_w: float32 [2, 4096, 4], P(None, 'ty')
- conv_b: float32 [2, 4096], P(None, 'ty')
- w_x: bfloat16 [2, 4096, 160], P(None, 'ty')
- w_dt: bfloat16 [2, 128, 4096], P(None, None, 'ty')
- dt_bias: float32 [2, 4096], P(None, 'ty')
- a_log: float32 [2, 4096, 16], P(None, 'ty')
- d_skip: float32 [2, 4096], P(None, 'ty')
- w_out: bfloat16 [2, 4096, 2048], P(None, 'ty', 'tx')
- conv_state: bfloat16 [2, 1024, 4096, 3], P(None, ('dp', 'tx'), 'ty')
- ssm_state: float32 [2, 1024, 4096, 16], P(None, ('dp', 'tx'), 'ty')
Outputs:
- output 1: float32 [1024, 2048], P('dp', 'tx')
- output 2: bfloat16 [2, 1024, 4096, 3], P(None, ('dp', 'tx'), 'ty')
- output 3: float32 [2, 1024, 4096, 16], P(None, ('dp', 'tx'), 'ty')
All inputs are finite; a program needn't handle non-finite values.
Results may differ from a plain program's by a relative error of at most 0.0181924.
Values are sent between devices in bfloat16 or wider.
A program may use at most 1 GiB of HBM per device.

v0:
```python
import jax
import jax.numpy as jnp
from jax import lax
from jax.sharding import PartitionSpec as P

NORM_EPS = 1e-5
INNER_EPS = 1e-6


def unit_rms(vec):
    return vec * lax.rsqrt(jnp.mean(vec * vec, axis=-1, keepdims=True) + INNER_EPS)


def channel_update(x_branch, z_branch, conv_prev, ssm_prev, conv_w, conv_b, w_x, w_dt, dt_bias, a_log, d_skip, reduce_fn):
    n_rank = w_dt.shape[0]
    n_state = a_log.shape[-1]
    window = jnp.concatenate([conv_prev, x_branch[:, :, None]], axis=-1)
    conv_val = jnp.sum(window.astype(jnp.float32) * conv_w, axis=-1) + conv_b
    x_conv = jax.nn.silu(conv_val).astype(jnp.bfloat16)
    x_dbl = reduce_fn(jnp.dot(x_conv, w_x, preferred_element_type=jnp.float32))
    dt_low = unit_rms(x_dbl[:, :n_rank])
    b_mat = unit_rms(x_dbl[:, n_rank:n_rank + n_state])
    c_mat = unit_rms(x_dbl[:, n_rank + n_state:])
    delta = jax.nn.softplus(jnp.dot(dt_low.astype(jnp.bfloat16), w_dt, preferred_element_type=jnp.float32) + dt_bias)
    x_float = x_conv.astype(jnp.float32)
    decay = jnp.exp(delta[:, :, None] * -jnp.exp(a_log))
    ssm_new = decay * ssm_prev + (delta * x_float)[:, :, None] * b_mat[:, None, :]
    state_val = jnp.sum(ssm_new * c_mat[:, None, :], axis=-1)
    gated = ((state_val + d_skip * x_float) * jax.nn.silu(z_branch.astype(jnp.float32))).astype(jnp.bfloat16)
    return gated, window[:, :, 1:], ssm_new


def solution(mesh):
    n_dmod = mesh.shape["tx"]

    def sum_over_ty(part_sum):
        return lax.psum(part_sum.astype(jnp.bfloat16), "ty").astype(jnp.float32)

    def local_step(residual, norm_w, w_in, conv_w, conv_b, w_x, w_dt, dt_bias, a_log, d_skip, w_out, conv_state, ssm_state):
        d_model = residual.shape[1] * n_dmod
        conv_list = []
        ssm_list = []
        for layer_idx in range(norm_w.shape[0]):
            sq_part = jnp.sum(residual * residual, axis=-1, keepdims=True)
            sq_total = lax.psum(sq_part, "tx")
            normed = (residual * lax.rsqrt(sq_total / d_model + NORM_EPS) * norm_w[layer_idx]).astype(jnp.bfloat16)
            proj_part = jnp.einsum("bd,dke->bke", normed, w_in[layer_idx], preferred_element_type=jnp.float32)
            proj_in = lax.psum_scatter(proj_part.astype(jnp.bfloat16), "tx", scatter_dimension=0, tiled=True)
            gated, conv_new, ssm_new = channel_update(proj_in[:, 0, :], proj_in[:, 1, :], conv_state[layer_idx], ssm_state[layer_idx], conv_w[layer_idx], conv_b[layer_idx], w_x[layer_idx], w_dt[layer_idx], dt_bias[layer_idx], a_log[layer_idx], d_skip[layer_idx], sum_over_ty)
            gated_rows = lax.all_gather(gated, "tx", axis=0, tiled=True)
            out_part = jnp.dot(gated_rows, w_out[layer_idx], preferred_element_type=jnp.float32)
            residual = residual + sum_over_ty(out_part)
            conv_list.append(conv_new)
            ssm_list.append(ssm_new)
        return residual, jnp.stack(conv_list), jnp.stack(ssm_list)

    cache_spec = P(None, ("dp", "tx"), "ty", None)
    in_specs = (P("dp", "tx"), P(None, "tx"), P(None, "tx", None, "ty"), P(None, "ty", None), P(None, "ty"), P(None, "ty", None), P(None, None, "ty"), P(None, "ty"), P(None, "ty", None), P(None, "ty"), P(None, "ty", "tx"), cache_spec, cache_spec)
    out_specs = (P("dp", "tx"), cache_spec, cache_spec)
    return jax.shard_map(local_step, mesh=mesh, in_specs=in_specs, out_specs=out_specs, check_vma=False)
```

profile of v0, /device:TPU:1, one launch (start us, length us, event | category | flops | bytes accessed | tf_op | source)
XLA Modules:
  0.0 509.6 jit_solution(1288697876254904004)
XLA Ops:
  7.2 0.8 slice_bitcast_fusion.9
  8.0 1.2 multiply_reduce_fusion.3
  9.2 35.5 %psum.42 = f32[1024,1]{0,1:T(1,128)S(1)} all-reduce(f32[1024,1]{0,1:T(1,128)S(1)} %bitcast.102), channel_id=1, replica_groups=mesh['dp'=1,'tx'=16,'ty'=8] {'tx'}, use_global_device_ids=true, to_apply=%region_1.0 | all-reduce | flops 1024 | bytes 8192 | tf_op jit(solution)/shard_map/psum | solution.py:45
  44.8 1.4 fusion.48
  46.2 3.2 convolution_convert_fusion.1
  49.7 76.9 %reduce-scatter.3.cloned.1.call-done = bf16[64,2,512]{2,0,1:T(8,128)(2,1)} async-done(((bf16[1024,2,512]{2,0,1:T(8,128)(2,1)}), bf16[64,2,512]{2,0,1:T(8,128)(2,1)}) %reduce-scatter.3.cloned.1.call-update) | async-done | bytes 131088 | tf_op jit(solution)/shard_map/reduce_scatter | solution.py:48
  126.6 0.8 slice_bitcast_fusion.5
  127.5 0.2 convolution_convert_fusion.5
  127.7 22.8 %psum.43 = bf16[64,160]{1,0:T(8,128)(2,1)S(1)} all-reduce(bf16[64,160]{1,0:T(8,128)(2,1)S(1)} %convolution_convert_fusion.5), channel_id=1, replica_groups=mesh['dp'=1,'tx'=16,'ty'=8] {'ty'}, use_global_device_ids=true, to_apply=%region_4.5 | all-reduce | flops 10240 | bytes 40960 | tf_op jit(solution)/shard_map/psum | solution.py:37
  151.0 0.3 convert_multiply_fusion.5
  151.3 2.5 fusion.5
  153.8 0.7 fusion.24
  154.6 40.2 %all-gather.3.cloned.1.call-done = bf16[1024,512]{1,0:T(8,128)(2,1)} async-done(((bf16[64,512]{1,0:T(8,128)(2,1)}), bf16[1024,512]{1,0:T(8,128)(2,1)}) %all-gather.3.cloned.1.call-update) | async-done | bytes 1048592 | tf_op jit(solution)/shard_map/all_gather | solution.py:50
  194.8 2.4 convolution_convert_fusion.3
  197.2 59.4 %all-reduce.3.cloned.1.call-done = bf16[1024,128]{1,0:T(8,128)(2,1)} async-done(((bf16[1024,128]{1,0:T(8,128)(2,1)}), bf16[1024,128]{1,0:T(8,128)(2,1)}) %all-reduce.3.cloned.1.call-update) | async-done | bytes 262160 | tf_op jit(solution)/shard_map/psum | solution.py:37
  256.7 1.2 multiply_reduce_fusion.1
  257.8 33.8 %psum.45 = f32[1024,1]{0,1:T(1,128)S(1)} all-reduce(f32[1024,1]{0,1:T(1,128)S(1)} %bitcast.103), channel_id=1, replica_groups=mesh['dp'=1,'tx'=16,'ty'=8] {'tx'}, use_global_device_ids=true, to_apply=%region_11.12 | all-reduce | flops 1024 | bytes 8192 | tf_op jit(solution)/shard_map/psum | solution.py:45
  291.6 3.0 convolution_convert_fusion
  294.7 76.5 %reduce-scatter.5.cloned.1.call-done = bf16[64,2,512]{2,0,1:T(8,128)(2,1)} async-done(((bf16[1024,2,512]{2,0,1:T(8,128)(2,1)}), bf16[64,2,512]{2,0,1:T(8,128)(2,1)}) %reduce-scatter.5.cloned.1.call-update) | async-done | bytes 131088 | tf_op jit(solution)/shard_map/reduce_scatter | solution.py:48
  371.2 0.8 slice_bitcast_fusion.3
  372.1 0.2 convolution_convert_fusion.4
  372.3 22.8 %psum.46 = bf16[64,160]{1,0:T(8,128)(2,1)S(1)} all-reduce(bf16[64,160]{1,0:T(8,128)(2,1)S(1)} %convolution_convert_fusion.4), channel_id=1, replica_groups=mesh['dp'=1,'tx'=16,'ty'=8] {'ty'}, use_global_device_ids=true, to_apply=%region_14.15 | all-reduce | flops 10240 | bytes 40960 | tf_op jit(solution)/shard_map/psum | solution.py:37
  395.5 0.3 convert_multiply_fusion.3
  395.8 2.5 fusion.2
  398.3 0.7 fusion.27
  399.1 2.7 multiply_add_fusion.1
  401.8 2.5 pad_maximum_fusion
  404.3 35.0 %all-gather.5.cloned.1.call-done = bf16[1024,512]{1,0:T(8,128)(2,1)} async-done(((bf16[64,512]{1,0:T(8,128)(2,1)}), bf16[1024,512]{1,0:T(8,128)(2,1)}) %all-gather.5.cloned.1.call-update) | async-done | bytes 1048592 | tf_op jit(solution)/shard_map/all_gather | solution.py:50
  439.2 2.4 convolution_convert_fusion.2
  441.7 0.8 pad_maximum_fusion.1
  442.4 58.5 %all-reduce.5.cloned.1.call-done = bf16[1024,128]{1,0:T(8,128)(2,1)} async-done(((bf16[1024,128]{1,0:T(8,128)(2,1)}), bf16[1024,128]{1,0:T(8,128)(2,1)}) %all-reduce.5.cloned.1.call-update) | async-done | bytes 262160 | tf_op jit(solution)/shard_map/psum | solution.py:37
  501.0 1.8 convert_add_fusion
  (63 shorter events, 1.5 us)
Async XLA Ops:
  7.2 119.5 %reduce-scatter.3.cloned.1.call-start = ((), (), s32[]{:S(2)}) async-start(), calls=%async_computation.2 | async-start | bytes 2228224 | tf_op jit(solution)/shard_map/reduce_scatter | solution.py:48
  46.2 3.3 copy-start.8
  46.2 3.3 copy-start.9
  46.2 3.4 copy-start.10
  46.2 3.4 copy-start.7
  46.2 3.4 copy-start.6
  46.2 3.4 copy-start.2
  49.4 78.1 %copy-start.11 = (bf16[2,512,160]{1,2,0:T(8,128)(2,1)S(1)}, bf16[2,512,160]{1,2,0:T(8,128)(2,1)}, u32[]{:S(2)}) copy-start(bf16[2,512,160]{1,2,0:T(8,128)(2,1)} %param.18) | copy-start | bytes 983044
  49.4 101.6 %copy-start.12 = (bf16[2,128,512]{2,1,0:T(8,128)(2,1)S(1)}, bf16[2,128,512]{2,1,0:T(8,128)(2,1)}, u32[]{:S(2)}) copy-start(bf16[2,128,512]{2,1,0:T(8,128)(2,1)} %param.19) | copy-start | bytes 786436
  49.5 145.3 %all-gather.3.cloned.1.call-start = ((), (), s32[]{:S(2)}) async-start(), calls=%async_computation.3 | async-start | bytes 1114112 | tf_op jit(solution)/shard_map/all_gather | solution.py:50
  127.7 26.1 %copy-start.4 = (bf16[64,2,512]{2,0,1:T(8,128)(2,1)S(1)}, bf16[64,2,512]{2,0,1:T(8,128)(2,1)}, u32[]{:S(2)}) copy-start(bf16[64,2,512]{2,0,1:T(8,128)(2,1)} %reduce-scatter.3.cloned.1.call-done) | copy-start | bytes 393220
  151.0 43.8 %copy-start.3 = (bf16[2,512,128]{2,1,0:T(8,128)(2,1)S(1)}, bf16[2,512,128]{2,1,0:T(8,128)(2,1)}, u32[]{:S(2)}) copy-start(bf16[2,512,128]{2,1,0:T(8,128)(2,1)} %param.23) | copy-start | bytes 786436
  151.3 105.4 %copy-start = (f32[1024,128]{1,0:T(8,128)S(1)}, f32[1024,128]{1,0:T(8,128)}, u32[]{:S(2)}) copy-start(f32[1024,128]{1,0:T(8,128)} %param.13) | copy-start | bytes 1572868
  154.6 102.1 %all-reduce.3.cloned.1.call-start = ((), (), s32[]{:S(2)}) async-start(), calls=%async_computation.4 | async-start | bytes 524288 | tf_op jit(solution)/shard_map/psum | solution.py:37
  197.2 174.0 %reduce-scatter.5.cloned.1.call-start = ((), (), s32[]{:S(2)}) async-start(), calls=%async_computation.5 | async-start | bytes 2228224 | tf_op jit(solution)/shard_map/reduce_scatter | solution.py:48
  294.7 144.6 %all-gather.5.cloned.1.call-start = ((), (), s32[]{:S(2)}) async-start(), calls=%async_computation.6 | async-start | bytes 1114112 | tf_op jit(solution)/shard_map/all_gather | solution.py:50
  372.3 26.0 %copy-start.5 = (bf16[64,2,512]{2,0,1:T(8,128)(2,1)S(1)}, bf16[64,2,512]{2,0,1:T(8,128)(2,1)}, u32[]{:S(2)}) copy-start(bf16[64,2,512]{2,0,1:T(8,128)(2,1)} %reduce-scatter.5.cloned.1.call-done) | copy-start | bytes 393220
  399.0 101.9 %all-reduce.5.cloned.1.call-start = ((), (), s32[]{:S(2)}) async-start(), calls=%async_computation.7 | async-start | bytes 524288 | tf_op jit(solution)/shard_map/psum | solution.py:37
  404.3 96.7 %copy-start.1 = (bf16[1024,128]{1,0:T(8,128)(2,1)S(1)}, bf16[1024,128]{1,0:T(8,128)(2,1)}, u32[]{:S(2)}) copy-start(bf16[1024,128]{1,0:T(8,128)(2,1)} %all-reduce.3.cloned.1.call-done) | copy-start | bytes 786436
Sparse Core Ops, SparseCore 0:
  49.6 77.0 reduce-scatter.2
  154.7 40.0 all-gather.2
  197.7 58.9 all-reduce.2
  294.8 76.3 reduce-scatter.4
  399.2 40.0 all-gather.4
  442.0 58.9 all-reduce.4
where the time goes:
time: 512 us; the launch traced here: 510 us
  waiting for transfers between devices  347 us (68%)
  blocking collectives  115 us (22%)
  other arithmetic  17.6 us (3%)
  between operations  14.5 us (3%)
  matrix products  11.9 us (2%)
    reduce_scatter x2, waiting for transfers between devices, local_step(): lax.psum_scatter(proj_part.astype(jnp.bfloat16), 'tx', scatter_dimension=...  153 us
    psum x2, waiting for transfers between devices, sum_over_ty(): return lax.psum(part_sum.astype(jnp.bfloat16), 'ty').astype(jnp.float32)  118 us
    all_gather x2, waiting for transfers between devices, local_step(): gated_rows = lax.all_gather(gated, 'tx', axis=0, tiled=True)  75.1 us
    psum x2, blocking collectives, local_step(): sq_total = lax.psum(sq_part, 'tx')  69.3 us
    psum x2, blocking collectives, sum_over_ty(): return lax.psum(part_sum.astype(jnp.bfloat16), 'ty').astype(jnp.float32)  45.6 us
  transfers between devices with their start and end apart: 6, of which 6 were waited for; matrix products, arithmetic and copies ran while one was open for 1% of the time, Pallas kernels for 0%

commit v1 on v0

v1 whole, which is shorter than its diff:
```python
import functools

import jax
import jax.numpy as jnp
from jax import lax
from jax.experimental import pallas as pl
from jax.experimental.pallas import tpu as pltpu
from jax.sharding import PartitionSpec as P

NORM_EPS = 1e-5
INNER_EPS = 1e-6
MESH = pl.DeviceIdType.MESH
F32 = jnp.float32
BF16 = jnp.bfloat16
LANES = 128


def nt_dot(lhs, rhs, precision=None):
    return lax.dot_general(lhs, rhs, (((1,), (1,)), ((), ())), precision=precision, preferred_element_type=F32)


def nn_dot(lhs, rhs):
    return jnp.dot(lhs, rhs, preferred_element_type=F32)


def unit_rms(vec, count):
    return vec * lax.rsqrt(jnp.sum(vec * vec, axis=-1, keepdims=True) / count + INNER_EPS)


def step_kernel(dims, res_ref, norm_ref, win_ref, cw_ref, cb_ref, wx_ref, wdt_ref, dtb_ref, al_ref, dsk_ref, wo_ref, cs_ref, ssm_in,
                res_out, conv_out, ssm_out,
                send_a, recv_a, send_b, recv_b, send_a2, recv_a2, send_b2, recv_b2, st_send, st_recv, st2_send, st2_recv, stat_t,
                p_send, p_recv, y_a, y_b, o_send, o_recv, sum_buf, ssm_buf, res_buf, dt_buf, dx_buf, bc_buf, yv_buf, xc_buf,
                a_ss, a_rs, b_ss, b_rs, a2_ss, a2_rs, b2_ss, b2_rs, st_ss, st_rs, st2_ss, st2_rs, p_ss, p_rs,
                ya_ss, ya_rs, yb_ss, yb_rs, ya2_ss, ya2_rs, yb2_ss, yb2_rs, o_ss, o_rs, s_ss, s_rs, ssm_is, ssm_os):
    n_z, n_y, n_ty, rows, layers, d_model, n_state, rank = dims
    tx, ty = lax.axis_index("tx"), lax.axis_index("ty")
    zi, yi = tx // n_y, tx % n_y
    chans = win_ref.shape[-1]
    half = chans // 2
    own_rows = o_recv.shape[2]
    pk = p_send.shape[1] - rows

    def y_peer(off):
        return lax.rem(yi + off, n_y)

    def z_peer(off):
        return lax.rem(zi + off, n_z)

    def at_y(off):
        return {"tx": zi * n_y + y_peer(off), "ty": ty}

    def at_z(off):
        return {"tx": z_peer(off) * n_y + yi, "ty": ty}

    def at_ty(idx):
        return {"tx": tx, "ty": idx}

    pending = []

    def copy(src, dst, ssem, rsem, device):
        return pltpu.make_async_remote_copy(src_ref=src, dst_ref=dst, send_sem=ssem, recv_sem=rsem, device_id=device, device_id_type=MESH)

    def send(src, dst, ssem, rsem, device):
        desc = copy(src, dst, ssem, rsem, device)
        desc.start()
        pending.append(desc)
        return desc

    for lyr in range(layers):
        pltpu.make_async_copy(ssm_in.at[lyr], ssm_buf.at[lyr], ssm_is.at[lyr]).start()

    barrier = pltpu.get_barrier_semaphore()
    for off in range(1, n_y):
        pl.semaphore_signal(barrier, inc=1, device_id=at_y(off), device_id_type=MESH)
    for off in range(1, n_z):
        pl.semaphore_signal(barrier, inc=1, device_id=at_z(off), device_id_type=MESH)
    for off in range(1, n_ty):
        pl.semaphore_signal(barrier, inc=1, device_id=at_ty(lax.rem(ty + off, n_ty)), device_id_type=MESH)
    pl.semaphore_wait(barrier, n_y + n_z + n_ty - 3)

    group = n_y * rows

    def input_matmul(lyr, source):
        ones = jnp.ones((8, LANES), F32)
        norm = norm_ref[lyr:lyr + 1, :]
        hidden = []
        for zz in range(n_z):
            res = source[zz * group:(zz + 1) * group, :]
            st_send[lyr, zz] = nt_dot(ones, res * res, lax.Precision.HIGHEST)
            hidden.append((res * norm).astype(BF16))
        for part in range(2):
            weight = win_ref[lyr, part]
            for zz in range(n_z):
                prod = nn_dot(hidden[zz], weight).astype(BF16)
                send_b[lyr, part, zz] = prod[:, half:]
                for yy in range(n_y):
                    send_a[lyr, part, yy, zz * rows:(zz + 1) * rows, :] = prod[yy * rows:(yy + 1) * rows, :half]
            if part == 0:
                phase_one(lyr, 0)

    def phase_one(lyr, part):
        for off in range(1, n_y):
            send(send_a.at[lyr, part, y_peer(off)], recv_a.at[lyr, part, off - 1], a_ss.at[lyr, part, off - 1], a_rs.at[lyr, part, off - 1], at_y(off))
        for off in range(1, n_z):
            if part == 0:
                send(st_send.at[lyr, z_peer(off)], st_recv.at[lyr, off - 1], st_ss.at[lyr, off - 1], st_rs.at[lyr, off - 1], at_z(off))
            send(send_b.at[lyr, part, z_peer(off)], recv_b.at[lyr, part, off - 1], b_ss.at[lyr, part, off - 1], b_rs.at[lyr, part, off - 1], at_z(off))

    def await_recv(src, dst, ssem, rsem, device):
        copy(src, dst, ssem, rsem, device).wait_recv()

    def phase_two(lyr, part):
        for off in range(1, n_z):
            if part == 0:
                await_recv(st_send.at[lyr, 0], st_recv.at[lyr, off - 1], st_ss.at[lyr, off - 1], st_rs.at[lyr, off - 1], at_z(off))
        if part == 0:
            st2_send[lyr] = functools.reduce(jnp.add, [st_recv[lyr, off - 1] for off in range(1, n_z)], st_send[lyr, zi])
            for off in range(1, n_y):
                send(st2_send.at[lyr], st2_recv.at[lyr, off - 1], st2_ss.at[lyr, off - 1], st2_rs.at[lyr, off - 1], at_y(off))
        for off in range(1, n_y):
            await_recv(send_a.at[lyr, part, 0], recv_a.at[lyr, part, off - 1], a_ss.at[lyr, part, off - 1], a_rs.at[lyr, part, off - 1], at_y(off))
        for zz in range(n_z):
            span = slice(zz * rows, (zz + 1) * rows)
            total = functools.reduce(jnp.add, [recv_a[lyr, part, off - 1, span, :].astype(F32) for off in range(1, n_y)], send_a[lyr, part, yi, span, :].astype(F32))
            send_a2[lyr, part, zz] = total.astype(BF16)
        for off in range(1, n_z):
            send(send_a2.at[lyr, part, z_peer(off)], recv_a2.at[lyr, part, off - 1], a2_ss.at[lyr, part, off - 1], a2_rs.at[lyr, part, off - 1], at_z(off))
        for off in range(1, n_z):
            await_recv(send_b.at[lyr, part, 0], recv_b.at[lyr, part, off - 1], b_ss.at[lyr, part, off - 1], b_rs.at[lyr, part, off - 1], at_z(off))
        for yy in range(n_y):
            span = slice(yy * rows, (yy + 1) * rows)
            total = functools.reduce(jnp.add, [recv_b[lyr, part, off - 1, span, :].astype(F32) for off in range(1, n_z)], send_b[lyr, part, zi, span, :].astype(F32))
            send_b2[lyr, part, yy] = total.astype(BF16)
        for off in range(1, n_y):
            send(send_b2.at[lyr, part, y_peer(off)], recv_b2.at[lyr, part, off - 1], b2_ss.at[lyr, part, off - 1], b2_rs.at[lyr, part, off - 1], at_y(off))

    def finish_sum(lyr, part):
        for off in range(1, n_z):
            await_recv(send_a2.at[lyr, part, 0], recv_a2.at[lyr, part, off - 1], a2_ss.at[lyr, part, off - 1], a2_rs.at[lyr, part, off - 1], at_z(off))
        for off in range(1, n_y):
            await_recv(send_b2.at[lyr, part, 0], recv_b2.at[lyr, part, off - 1], b2_ss.at[lyr, part, off - 1], b2_rs.at[lyr, part, off - 1], at_y(off))
        tot_a = functools.reduce(jnp.add, [recv_a2[lyr, part, off - 1].astype(F32) for off in range(1, n_z)], send_a2[lyr, part, zi].astype(F32))
        tot_b = functools.reduce(jnp.add, [recv_b2[lyr, part, off - 1].astype(F32) for off in range(1, n_y)], send_b2[lyr, part, yi].astype(F32))
        return jnp.concatenate([tot_a, tot_b], axis=-1)

    def row_scale(lyr):
        for off in range(1, n_y):
            await_recv(st2_send.at[lyr], st2_recv.at[lyr, off - 1], st2_ss.at[lyr, off - 1], st2_rs.at[lyr, off - 1], at_y(off))
        total = functools.reduce(jnp.add, [st2_recv[lyr, off - 1] for off in range(1, n_y)], st2_send[lyr])
        stat_t[...] = total.T
        mine = stat_t[pl.ds(pl.multiple_of(yi * rows, 8), rows), :][:, :1]
        return lax.rsqrt(mine / d_model + NORM_EPS)

    source = res_ref
    for lyr in range(layers):
        input_matmul(lyr, source)
        phase_two(lyr, 0)
        phase_one(lyr, 1)
        scale = row_scale(lyr)
        x_in = (finish_sum(lyr, 0) * scale).astype(BF16)

        taps = [cs_ref[lyr, k] for k in range(3)]
        conv_out[lyr, 0] = taps[1]
        conv_out[lyr, 1] = taps[2]
        conv_out[lyr, 2] = x_in
        conv = x_in.astype(F32) * cw_ref[lyr, 3:4, :] + cb_ref[lyr:lyr + 1, :]
        for k in range(3):
            conv = conv + taps[k].astype(F32) * cw_ref[lyr, k:k + 1, :]
        x_conv = (conv * jax.nn.sigmoid(conv)).astype(BF16)

        wx = wx_ref[lyr]
        dt_part = nt_dot(x_conv, wx[:rank])
        bc_w = jnp.concatenate([wx[rank:], jnp.zeros((LANES - 2 * n_state, chans), BF16)], axis=0)
        bc_part = nt_dot(x_conv, bc_w)
        packs = rows // pk
        shift = LANES // packs
        packed = bc_part[:pk]
        for q in range(1, packs):
            packed = packed + pltpu.roll(bc_part[q * pk:(q + 1) * pk], q * shift, 1)
        p_send[lyr, :rows] = dt_part.astype(BF16)
        p_send[lyr, rows:] = packed.astype(BF16)
        for off in range(1, n_ty):
            send(p_send.at[lyr], p_recv.at[lyr, off - 1], p_ss.at[lyr, off - 1], p_rs.at[lyr, off - 1], at_ty(lax.rem(ty + off, n_ty)))

        phase_two(lyr, 1)

        for off in range(1, n_ty):
            await_recv(p_send.at[lyr], p_recv.at[lyr, off - 1], p_ss.at[lyr, off - 1], p_rs.at[lyr, off - 1], at_ty(ty))
        proj = functools.reduce(jnp.add, [p_recv[lyr, off - 1].astype(F32) for off in range(1, n_ty)], p_send[lyr].astype(F32))
        dt_low = unit_rms(proj[:rows], rank).astype(BF16)
        lane = lax.broadcasted_iota(jnp.int32, (pk, LANES), 1)
        for q in range(packs):
            piece = proj[rows:]
            if q:
                piece = pltpu.roll(piece, LANES - q * shift, 1)
            sq = piece * piece
            b_inv = lax.rsqrt(jnp.sum(jnp.where(lane < n_state, sq, 0.0), axis=-1, keepdims=True) / n_state + INNER_EPS)
            c_inv = lax.rsqrt(jnp.sum(jnp.where((lane >= n_state) & (lane < 2 * n_state), sq, 0.0), axis=-1, keepdims=True) / n_state + INNER_EPS)
            bc_buf[q * pk:(q + 1) * pk] = piece * jnp.where(lane < n_state, b_inv, c_inv)
        raw = nn_dot(dt_low, wdt_ref[lyr]) + dtb_ref[lyr:lyr + 1, :]
        delta = jnp.maximum(raw, 0.0) + jnp.log1p(jnp.exp(-jnp.abs(raw)))
        dt_buf[...] = delta
        dx_buf[...] = delta * x_conv.astype(F32)
        xc_buf[...] = x_conv

        pltpu.make_async_copy(ssm_in.at[lyr], ssm_buf.at[lyr], ssm_is.at[lyr]).wait()
        neg_a = -jnp.exp(al_ref[lyr])

        def update(grp, carry):
            base = pl.multiple_of(grp * 8, 8)
            d_rows = dt_buf[pl.ds(base, 8), :]
            x_rows = dx_buf[pl.ds(base, 8), :]
            bc_t = bc_buf[pl.ds(base, 8), :].T
            outs = []
            for j in range(8):
                decay = jnp.exp(d_rows[j:j + 1, :] * neg_a)
                state = decay * ssm_buf[lyr, base + j] + x_rows[j:j + 1, :] * bc_t[:n_state, j:j + 1]
                ssm_buf[lyr, base + j] = state
                outs.append(jnp.sum(state * bc_t[n_state:2 * n_state, j:j + 1], axis=0, keepdims=True))
            yv_buf[pl.ds(base, 8), :] = jnp.concatenate(outs, axis=0)
            return carry

        lax.fori_loop(0, rows // 8, update, 0)
        pltpu.make_async_copy(ssm_buf.at[lyr], ssm_out.at[lyr], ssm_os.at[lyr]).start()

        z_in = (finish_sum(lyr, 1) * scale).astype(BF16).astype(F32)
        gated = ((yv_buf[...] + dsk_ref[lyr:lyr + 1, :] * xc_buf[...].astype(F32)) * (z_in * jax.nn.sigmoid(z_in))).astype(BF16)
        y_a[lyr, zi, yi] = gated[:, :half]
        y_b[lyr, zi, yi] = gated[:, half:]

        def push(buf, zz, yy, ssem, rsem, device):
            send(buf.at[lyr, zz, yy], buf.at[lyr, zz, yy], ssem, rsem, device)

        def landed(buf, ssem, rsem):
            await_recv(buf.at[lyr, 0, 0], buf.at[lyr, 0, 0], ssem, rsem, at_ty(ty))

        for off in range(1, n_y):
            push(y_a, zi, yi, ya_ss.at[lyr, off - 1], ya_rs.at[lyr, off - 1], at_y(off))
        for off in range(1, n_z):
            push(y_b, zi, yi, yb_ss.at[lyr, off - 1], yb_rs.at[lyr, off - 1], at_z(off))
        for out in range(1, n_z):
            push(y_a, zi, yi, ya2_ss.at[lyr, out - 1, 0], ya2_rs.at[lyr, out - 1, 0], at_z(out))
        for out in range(1, n_y):
            push(y_b, zi, yi, yb2_ss.at[lyr, out - 1, 0], yb2_rs.at[lyr, out - 1, 0], at_y(out))
        for off in range(1, n_y):
            landed(y_a, ya_ss.at[lyr, off - 1], ya_rs.at[lyr, off - 1])
            for out in range(1, n_z):
                push(y_a, zi, lax.rem(yi + n_y - off, n_y), ya2_ss.at[lyr, out - 1, off], ya2_rs.at[lyr, out - 1, off], at_z(out))
        for off in range(1, n_z):
            landed(y_b, yb_ss.at[lyr, off - 1], yb_rs.at[lyr, off - 1])
            for out in range(1, n_y):
                push(y_b, lax.rem(zi + n_z - off, n_z), yi, yb2_ss.at[lyr, out - 1, off], yb2_rs.at[lyr, out - 1, off], at_y(out))

        per_group = n_ty // n_z
        for off in range(n_z):
            zz = lax.rem(zi + n_z - off, n_z)
            if off:
                for oy in range(n_y):
                    landed(y_a, ya2_ss.at[lyr, off - 1, oy], ya2_rs.at[lyr, off - 1, oy])
            for oy in range(1, n_y):
                landed(y_b, yb2_ss.at[lyr, oy - 1, off], yb2_rs.at[lyr, oy - 1, off])
            part = nn_dot(y_a[lyr, zz].reshape(group, half), wo_ref[lyr, :half]) + nn_dot(y_b[lyr, zz].reshape(group, half), wo_ref[lyr, half:])
            for i in range(per_group):
                o_send[lyr, zz * per_group + i] = part[i * own_rows:(i + 1) * own_rows].astype(BF16)
            for i in range(per_group):
                owner = zz * per_group + i
                slot = lax.rem(owner - ty + n_ty - 1, n_ty)

                @pl.when(owner != ty)
                def _():
                    copy(o_send.at[lyr, owner], o_recv.at[lyr, slot], o_ss.at[lyr, slot], o_rs.at[lyr, slot], at_ty(owner)).start()

        for off in range(1, n_ty):
            await_recv(o_send.at[lyr, 0], o_recv.at[lyr, off - 1], o_ss.at[lyr, off - 1], o_rs.at[lyr, off - 1], at_ty(ty))
        total = functools.reduce(jnp.add, [o_recv[lyr, off - 1].astype(F32) for off in range(1, n_ty)], o_send[lyr, ty].astype(F32))
        sum_buf[lyr, ty] = total.astype(BF16)
        for off in range(1, n_ty):
            send(sum_buf.at[lyr, ty], sum_buf.at[lyr, ty], s_ss.at[lyr, off - 1], s_rs.at[lyr, off - 1], at_ty(lax.rem(ty + off, n_ty)))
        for off in range(1, n_ty):
            await_recv(sum_buf.at[lyr, 0], sum_buf.at[lyr, 0], s_ss.at[lyr, off - 1], s_rs.at[lyr, off - 1], at_ty(ty))
        target = res_out if lyr == layers - 1 else res_buf
        for blk in range(n_ty):
            span = slice(blk * own_rows, (blk + 1) * own_rows)
            target[span, :] = source[span, :] + sum_buf[lyr, blk].astype(F32)
        source = target

    for desc in pending:
        desc.wait_send()
    for lyr in range(layers):
        for off in range(1, n_ty):
            copy(o_send.at[lyr, 0], o_recv.at[lyr, off - 1], o_ss.at[lyr, off - 1], o_rs.at[lyr, off - 1], at_ty(ty)).wait_send()
        pltpu.make_async_copy(ssm_buf.at[lyr], ssm_out.at[lyr], ssm_os.at[lyr]).wait()


def build(mesh, n_y):
    n_tx, n_ty = mesh.shape["tx"], mesh.shape["ty"]
    n_z = n_tx // n_y

    def local_step(residual, norm_w, w_in, conv_w, conv_b, w_x, w_dt, dt_bias, a_log, d_skip, w_out, conv_state, ssm_state):
        layers, batch, chans, n_state = ssm_state.shape
        rows = batch
        all_rows, d_local = residual.shape
        rank = w_dt.shape[1]
        half = chans // 2
        own = all_rows // n_ty
        pk = rows * 2 * n_state // LANES
        dims = (n_z, n_y, n_ty, rows, layers, d_local * n_tx, n_state, rank)
        vmem = pl.BlockSpec(memory_space=pltpu.VMEM)
        anyspace = pl.BlockSpec(memory_space=pl.ANY)
        dma = pltpu.SemaphoreType.DMA
        scratch = [
            pltpu.VMEM((layers, 2, n_y, n_z * rows, half), BF16),
            pltpu.VMEM((layers, 2, n_y - 1, n_z * rows, half), BF16),
            pltpu.VMEM((layers, 2, n_z, n_y * rows, half), BF16),
            pltpu.VMEM((layers, 2, n_z - 1, n_y * rows, half), BF16),
            pltpu.VMEM((layers, 2, n_z, rows, half), BF16),
            pltpu.VMEM((layers, 2, n_z - 1, rows, half), BF16),
            pltpu.VMEM((layers, 2, n_y, rows, half), BF16),
            pltpu.VMEM((layers, 2, n_y - 1, rows, half), BF16),
            pltpu.VMEM((layers, n_z, 8, n_y * rows), F32),
            pltpu.VMEM((layers, n_z - 1, 8, n_y * rows), F32),
            pltpu.VMEM((layers, 8, n_y * rows), F32),
            pltpu.VMEM((layers, n_y - 1, 8, n_y * rows), F32),
            pltpu.VMEM((n_y * rows, 8), F32),
            pltpu.VMEM((layers, rows + pk, LANES), BF16),
            pltpu.VMEM((layers, n_ty - 1, rows + pk, LANES), BF16),
            pltpu.VMEM((layers, n_z, n_y, rows, half), BF16),
            pltpu.VMEM((layers, n_z, n_y, rows, half), BF16),
            pltpu.VMEM((layers, n_ty, own, d_local), BF16),
            pltpu.VMEM((layers, n_ty - 1, own, d_local), BF16),
            pltpu.VMEM((layers, n_ty, own, d_local), BF16),
            pltpu.VMEM((layers, rows, n_state, chans), F32),
            pltpu.VMEM((all_rows, d_local), F32),
            pltpu.VMEM((rows, chans), F32),
            pltpu.VMEM((rows, chans), F32),
            pltpu.VMEM((rows, LANES), F32),
            pltpu.VMEM((rows, chans), F32),
            pltpu.VMEM((rows, chans), BF16),
        ]
        y1, z1, t1 = n_y - 1, n_z - 1, n_ty - 1
        for shape in [(layers, 2, y1), (layers, 2, z1), (layers, 2, z1), (layers, 2, y1), (layers, z1), (layers, y1), (layers, t1),
                      (layers, y1), (layers, z1), (layers, z1, n_y), (layers, y1, n_z), (layers, t1), (layers, t1)]:
            scratch += [dma(shape), dma(shape)]
        scratch += [dma((layers,)), dma((layers,))]
        res, conv, ssm = pl.pallas_call(
            functools.partial(step_kernel, dims),
            out_shape=(
                jax.ShapeDtypeStruct(residual.shape, F32),
                jax.ShapeDtypeStruct((layers, 3, rows, chans), BF16),
                jax.ShapeDtypeStruct((layers, rows, n_state, chans), F32),
            ),
            in_specs=[vmem] * 12 + [anyspace],
            out_specs=(vmem, vmem, anyspace),
            scratch_shapes=scratch,
            compiler_params=pltpu.CompilerParams(collective_id=0, has_side_effects=True, vmem_limit_bytes=60 * 1024 * 1024),
        )(
            residual, norm_w, w_in.transpose(0, 2, 1, 3), conv_w.transpose(0, 2, 1), conv_b, w_x.transpose(0, 2, 1), w_dt, dt_bias,
            a_log.transpose(0, 2, 1), d_skip, w_out, conv_state.transpose(0, 3, 1, 2), ssm_state.transpose(0, 1, 3, 2),
        )
        return res, conv.transpose(0, 2, 3, 1), ssm.transpose(0, 1, 3, 2)

    cache_spec = P(None, ("dp", "tx"), "ty", None)
    in_specs = (P("dp", "tx"), P(None, "tx"), P(None, "tx", None, "ty"), P(None, "ty", None), P(None, "ty"), P(None, "ty", None), P(None, None, "ty"), P(None, "ty"), P(None, "ty", None), P(None, "ty"), P(None, "ty", "tx"), cache_spec, cache_spec)
    out_specs = (P("dp", "tx"), cache_spec, cache_spec)
    return jax.shard_map(local_step, mesh=mesh, in_specs=in_specs, out_specs=out_specs, check_vma=False)


def solution(mesh):
    return build(mesh, 4)
```

time: 512 us -> 109 us (0.21)
  waiting for transfers between devices: 347 us -> 0 us
  blocking collectives: 115 us -> 0 us
  Pallas kernels: 0 us -> 97.7 us
  other arithmetic: 17.6 us -> 0 us
  between operations: 14.5 us -> 0.64 us
  matrix products: 11.9 us -> 0 us
  local copies, waits for them, and re-layouts: 3.96 us -> 10.6 us
    reduce_scatter x2 -> x0, waiting for transfers between devices: 153 us -> none  [local_step(): lax.psum_scatter(proj_part.astype(jnp.bfloat16), 'tx', scatter_dimension=...]
    psum x2 -> x0, waiting for transfers between devices: 118 us -> none  [sum_over_ty(): return lax.psum(part_sum.astype(jnp.bfloat16), 'ty').astype(jnp.float32)]
    psum x4 -> x0, blocking collectives: 115 us -> none  [the longest x2 69.3 us: local_step(): sq_total = lax.psum(sq_part, 'tx')]
    pallas_call x0 -> x1, Pallas kernels: none -> 97.7 us  [local_step(): pl.pallas_call(functools.partial(step_kernel, dims), out_shape=(jax.Shape...]
    all_gather x2 -> x0, waiting for transfers between devices: 75.1 us -> none  [local_step(): gated_rows = lax.all_gather(gated, 'tx', axis=0, tiled=True)]
    dot_general x8 -> x0, matrix products: 11.9 us -> none  [the longest x2 6.21 us: local_step(): jnp.einsum('bd,dke->bke', normed, w_in[layer_idx], preferred_element_type...]
    unnamed x26 -> x4, local copies, waits for them, and re-layouts: 0.07 us -> 10.6 us
    reduce_sum x10 -> x0, other arithmetic: 8.04 us -> none  [the longest x2 4.96 us: channel_update(): state_val = jnp.sum(ssm_new * c_mat[:, None, :], axis=-1)]
  transfers between devices with their start and end apart: 6 -> 0, of which waited for: 6 -> 0; matrix products, arithmetic and copies ran while one was open for 1% -> 0% of each run, Pallas kernels for 0% -> 0%
where the time goes in v1:
time: 109 us
  Pallas kernels  97.7 us (90%)
  local copies, waits for them, and re-layouts  10.6 us (10%)
    pallas_call x1, Pallas kernels, local_step(): pl.pallas_call(functools.partial(step_kernel, dims), out_shape=(jax.Shape...  97.7 us
    unnamed x4, local copies, waits for them, and re-layouts  10.6 us

profile of v1, /device:TPU:1, one launch (start us, length us, event | category | flops | bytes accessed | tf_op | source)
XLA Modules:
  0.0 109.0 jit_solution(14769611744099175240)
XLA Ops:
  0.6 1.9 %copy.18 = bf16[2,128,2,512]{3,1,2,0:T(8,128)(2,1)} copy(bf16[2,128,2,512]{3,2,1,0:T(2,128)(2,1)} %param.15) | data formatting | bytes 1048576 | tf_op args[2]
  2.5 97.7 %shard_map.148 = (f32[1024,128]{1,0:T(8,128)}, bf16[2,3,64,512]{3,2,1,0:T(8,128)(2,1)}, f32[2,64,16,512]{3,2,1,0:T(8,128)}) custom-call(f32[1024,128]{1,0:T(8,128)} %res_ref.1, f32[2,128]{1,0:T(2,128)} %norm_ref.1, bf16[2,2,128,512]{3,2,1,0:T(8,128)(2,1)} %bitcast.12, f32[2,4,512]{2,1,0:T(4,128)} %bitcast.17, f32[2,512]{1,0:T(2,128)} %cb_ref.1, ...), custom_call_target="tpu_custom_call" | custom-call | tf_op jit(solution)/shard_map/pallas_call | solution.py:346
  100.3 1.9 %copy.22 = f32[1024,128]{1,0:T(8,128)} copy(f32[1024,128]{1,0:T(8,128)} %get-tuple-element.12) | data formatting | bytes 1048576
  102.1 1.8 %copy.23 = bf16[2,64,512,3]{2,1,3,0:T(8,128)(2,1)} copy(bf16[2,64,512,3]{2,1,3,0:T(8,128)(2,1)} %bitcast.14) | data formatting | bytes 786432
  103.9 5.0 %copy.24 = f32[2,64,512,16]{2,3,1,0:T(8,128)} copy(f32[2,64,512,16]{2,3,1,0:T(8,128)} %bitcast.11) | data formatting | bytes 8388608

commit v2 on v0

v2 whole, which is shorter than its diff:
```python
import functools

import jax
import jax.numpy as jnp
from jax import lax
from jax.experimental import pallas as pl
from jax.experimental.pallas import tpu as pltpu
from jax.sharding import PartitionSpec as P

NORM_EPS = 1e-5
INNER_EPS = 1e-6
MESH = pl.DeviceIdType.MESH
F32 = jnp.float32
BF16 = jnp.bfloat16
LANES = 128
VMEM_LIMIT = 52 * 1024 * 1024


def nt_dot(lhs, rhs, precision=None):
    return lax.dot_general(lhs, rhs, (((1,), (1,)), ((), ())), precision=precision, preferred_element_type=F32)


def nn_dot(lhs, rhs):
    return jnp.dot(lhs, rhs, preferred_element_type=F32)


def unit_rms(vec, count):
    return vec * lax.rsqrt(jnp.sum(vec * vec, axis=-1, keepdims=True) / count + INNER_EPS)


def step_kernel(dims, res_in, norm_in, win_in, cw_in, cb_in, wx_in, wdt_in, dtb_in, al_in, dsk_in, wo_in, cs_in, ssm_in,
                res_out, conv_out, ssm_buf,
                res_ref, norm_ref, win_ref, cw_ref, cb_ref, wx_ref, wdt_ref, dtb_ref, al_ref, dsk_ref, wo_ref, cs_ref,
                w_buf, send_a, recv_a, send_b, recv_b, send_a2, recv_a2, send_b2, recv_b2, st_send, st_recv, st2_send, st2_recv, stat_t,
                p_send, p_recv, y_a, y_b, o_send, o_recv, sum_buf, res_buf, dt_buf, dx_buf, bc_buf, yv_buf, xc_buf,
                a_ss, a_rs, b_ss, b_rs, a2_ss, a2_rs, b2_ss, b2_rs, st_ss, st_rs, st2_ss, st2_rs, p_ss, p_rs,
                ya_ss, ya_rs, yb_ss, yb_rs, ya2_ss, ya2_rs, yb2_ss, yb2_rs, o_ss, o_rs, s_ss, s_rs, in_sems):
    n_z, n_y, n_ty, n_str, rows, layers, d_model, n_state, rank, lag = dims
    tx, ty = lax.axis_index("tx"), lax.axis_index("ty")
    zi, yi = tx // n_y, tx % n_y
    chans = win_ref.shape[-1]
    half = chans // 2
    own_blocks = n_z * n_y // n_ty
    own_rows = own_blocks * rows
    group = n_y * rows
    pk = p_send.shape[1] - rows
    scope = jax.named_scope

    def y_peer(off):
        return lax.rem(yi + off, n_y)

    def z_peer(off):
        return lax.rem(zi + off, n_z)

    def at_y(off):
        return {"tx": zi * n_y + y_peer(off), "ty": ty}

    def at_z(off):
        return {"tx": z_peer(off) * n_y + yi, "ty": ty}

    def at_ty(idx):
        return {"tx": tx, "ty": idx}

    def ty_peer(off):
        return at_ty(lax.rem(ty + off, n_ty))

    pending = []

    def copy(src, dst, ssem, rsem, device):
        return pltpu.make_async_remote_copy(src_ref=src, dst_ref=dst, send_sem=ssem, recv_sem=rsem, device_id=device, device_id_type=MESH)

    def send(src, dst, ssem, rsem, device):
        desc = copy(src, dst, ssem, rsem, device)
        desc.start()
        pending.append(desc)

    def await_recv(src, dst, ssem, rsem, device):
        copy(src, dst, ssem, rsem, device).wait_recv()

    def add_up(first, others):
        return functools.reduce(jnp.add, [o.astype(F32) for o in others], first.astype(F32))

    def input_matmul(k, lyr, strm, source, part):
        norm = norm_ref[lyr:lyr + 1, :]
        for zz in range(n_z):
            res = source[zz * n_y:(zz + 1) * n_y, strm].reshape(group, LANES)
            if part == 0:
                st_send[k, zz] = nt_dot(jnp.ones((8, LANES), F32), res * res, lax.Precision.HIGHEST)
            prod = nn_dot((res * norm).astype(BF16), w_buf[lyr, part]).astype(BF16)
            send_b[k, part, zz] = prod[:, half:]
            for yy in range(n_y):
                send_a[k, part, yy, zz * rows:(zz + 1) * rows, :] = prod[yy * rows:(yy + 1) * rows, :half]

    def phase_one(k, part):
        for off in range(1, n_z):
            if part == 0:
                send(st_send.at[k, z_peer(off)], st_recv.at[k, off - 1], st_ss.at[k, off - 1], st_rs.at[k, off - 1], at_z(off))
        for off in range(1, max(n_y, n_z)):
            if off < n_y:
                send(send_a.at[k, part, y_peer(off)], recv_a.at[k, part, off - 1], a_ss.at[k, part, off - 1], a_rs.at[k, part, off - 1], at_y(off))
            if off < n_z:
                send(send_b.at[k, part, z_peer(off)], recv_b.at[k, part, off - 1], b_ss.at[k, part, off - 1], b_rs.at[k, part, off - 1], at_z(off))

    def phase_two(k, part):
        if part == 0:
            for off in range(1, n_z):
                await_recv(st_send.at[k, 0], st_recv.at[k, off - 1], st_ss.at[k, off - 1], st_rs.at[k, off - 1], at_z(off))
            st2_send[k] = add_up(st_send[k, zi], [st_recv[k, off - 1] for off in range(1, n_z)])
            for off in range(1, n_y):
                send(st2_send.at[k], st2_recv.at[k, off - 1], st2_ss.at[k, off - 1], st2_rs.at[k, off - 1], at_y(off))
        with scope(f"wait_a1_{part}"):
            for off in range(1, n_y):
                await_recv(send_a.at[k, part, 0], recv_a.at[k, part, off - 1], a_ss.at[k, part, off - 1], a_rs.at[k, part, off - 1], at_y(off))
        for zz in range(n_z):
            span = slice(zz * rows, (zz + 1) * rows)
            send_a2[k, part, zz] = add_up(send_a[k, part, yi, span, :], [recv_a[k, part, off - 1, span, :] for off in range(1, n_y)]).astype(BF16)
        for off in range(1, n_z):
            send(send_a2.at[k, part, z_peer(off)], recv_a2.at[k, part, off - 1], a2_ss.at[k, part, off - 1], a2_rs.at[k, part, off - 1], at_z(off))
        with scope(f"wait_b1_{part}"):
            for off in range(1, n_z):
                await_recv(send_b.at[k, part, 0], recv_b.at[k, part, off - 1], b_ss.at[k, part, off - 1], b_rs.at[k, part, off - 1], at_z(off))
        for yy in range(n_y):
            span = slice(yy * rows, (yy + 1) * rows)
            send_b2[k, part, yy] = add_up(send_b[k, part, zi, span, :], [recv_b[k, part, off - 1, span, :] for off in range(1, n_z)]).astype(BF16)
        for off in range(1, n_y):
            send(send_b2.at[k, part, y_peer(off)], recv_b2.at[k, part, off - 1], b2_ss.at[k, part, off - 1], b2_rs.at[k, part, off - 1], at_y(off))

    def finish_sum(k, part):
        with scope(f"wait_2_{part}"):
            for off in range(1, n_z):
                await_recv(send_a2.at[k, part, 0], recv_a2.at[k, part, off - 1], a2_ss.at[k, part, off - 1], a2_rs.at[k, part, off - 1], at_z(off))
            for off in range(1, n_y):
                await_recv(send_b2.at[k, part, 0], recv_b2.at[k, part, off - 1], b2_ss.at[k, part, off - 1], b2_rs.at[k, part, off - 1], at_y(off))
        tot_a = add_up(send_a2[k, part, zi], [recv_a2[k, part, off - 1] for off in range(1, n_z)])
        tot_b = add_up(send_b2[k, part, yi], [recv_b2[k, part, off - 1] for off in range(1, n_y)])
        return jnp.concatenate([tot_a, tot_b], axis=-1)

    def row_scale(k):
        for off in range(1, n_y):
            await_recv(st2_send.at[k], st2_recv.at[k, off - 1], st2_ss.at[k, off - 1], st2_rs.at[k, off - 1], at_y(off))
        stat_t[k] = add_up(st2_send[k], [st2_recv[k, off - 1] for off in range(1, n_y)]).T
        mine = stat_t[k, pl.ds(pl.multiple_of(yi * rows, 8), rows), :][:, :1]
        return lax.rsqrt(mine / d_model + NORM_EPS)

    def conv_and_proj(k, lyr, mine, x_in):
        taps = [cs_ref[lyr, j, mine, :] for j in range(3)]
        conv_out[lyr, 0, mine, :] = taps[1]
        conv_out[lyr, 1, mine, :] = taps[2]
        conv_out[lyr, 2, mine, :] = x_in
        conv = x_in.astype(F32) * cw_ref[lyr, 3:4, :] + cb_ref[lyr:lyr + 1, :]
        for j in range(3):
            conv = conv + taps[j].astype(F32) * cw_ref[lyr, j:j + 1, :]
        x_conv = (conv * jax.nn.sigmoid(conv)).astype(BF16)
        xc_buf[k] = x_conv
        wx = wx_ref[lyr]
        bc_w = jnp.concatenate([wx[rank:], jnp.zeros((LANES - 2 * n_state, chans), BF16)], axis=0)
        bc_part = nt_dot(x_conv, bc_w)
        packed = bc_part[:pk]
        for q in range(1, rows // pk):
            packed = packed + pltpu.roll(bc_part[q * pk:(q + 1) * pk], q * 2 * n_state, 1)
        p_send[k, :rows] = nt_dot(x_conv, wx[:rank]).astype(BF16)
        p_send[k, rows:] = packed.astype(BF16)

    def step_sizes(k, lyr):
        proj = add_up(p_send[k], [p_recv[k, off - 1] for off in range(1, n_ty)])
        dt_low = unit_rms(proj[:rows], rank).astype(BF16)
        lane = lax.broadcasted_iota(jnp.int32, (pk, LANES), 1)
        for q in range(rows // pk):
            piece = proj[rows:]
            if q:
                piece = pltpu.roll(piece, LANES - q * 2 * n_state, 1)
            sq = piece * piece
            b_inv = lax.rsqrt(jnp.sum(jnp.where(lane < n_state, sq, 0.0), axis=-1, keepdims=True) / n_state + INNER_EPS)
            c_inv = lax.rsqrt(jnp.sum(jnp.where((lane >= n_state) & (lane < 2 * n_state), sq, 0.0), axis=-1, keepdims=True) / n_state + INNER_EPS)
            bc_buf[k, q * pk:(q + 1) * pk] = piece * jnp.where(lane < n_state, b_inv, c_inv)
        raw = nn_dot(dt_low, wdt_ref[lyr]) + dtb_ref[lyr:lyr + 1, :]
        delta = jnp.maximum(raw, 0.0) + jnp.log1p(jnp.exp(-jnp.abs(raw)))
        dt_buf[k] = delta
        dx_buf[k] = delta * xc_buf[k].astype(F32)

    def state_update(k, lyr, strm):
        neg_a = -jnp.exp(al_ref[lyr])

        def update(grp, carry):
            base = pl.multiple_of(grp * 8, 8)
            d_rows = dt_buf[k, pl.ds(base, 8), :]
            x_rows = dx_buf[k, pl.ds(base, 8), :]
            bc_t = bc_buf[k, pl.ds(base, 8), :].T
            outs = []
            for j in range(8):
                row = strm * rows + base + j
                decay = jnp.exp(d_rows[j:j + 1, :] * neg_a)
                state = decay * ssm_buf[lyr, row] + x_rows[j:j + 1, :] * bc_t[:n_state, j:j + 1]
                ssm_buf[lyr, row] = state
                outs.append(jnp.sum(state * bc_t[n_state:2 * n_state, j:j + 1], axis=0, keepdims=True))
            yv_buf[k, pl.ds(base, 8), :] = jnp.concatenate(outs, axis=0)
            return carry

        lax.fori_loop(0, rows // 8, update, 0)

    def push(buf, k, zz, yy, ssem, rsem, device):
        send(buf.at[k, zz, yy], buf.at[k, zz, yy], ssem, rsem, device)

    def landed(buf, k, ssem, rsem):
        await_recv(buf.at[k, 0, 0], buf.at[k, 0, 0], ssem, rsem, at_ty(ty))

    def stream(strm):
        mine = slice(strm * rows, (strm + 1) * rows)
        source = res_ref
        for lyr in range(layers):
            k = lyr * n_str + strm
            with scope(f"matmul_{strm}"):
                input_matmul(k, lyr, strm, source, 0)
            if lyr == 0:
                input_matmul(k, lyr, strm, source, 1)
                yield
            phase_one(k, 0)
            if lyr:
                input_matmul(k, lyr, strm, source, 1)
            yield
            with scope(f"phase2_{strm}"):
                phase_two(k, 0)
            phase_one(k, 1)
            yield
            with scope(f"xconv_{strm}"):
                scale = row_scale(k)
                need(7)
                conv_and_proj(k, lyr, mine, (finish_sum(k, 0) * scale).astype(BF16))
            for off in range(1, n_ty):
                send(p_send.at[k], p_recv.at[k, off - 1], p_ss.at[k, off - 1], p_rs.at[k, off - 1], ty_peer(off))
            yield
            with scope(f"phase2z_{strm}"):
                phase_two(k, 1)
            yield
            with scope(f"wait_p_{strm}"):
                for off in range(1, n_ty):
                    await_recv(p_send.at[k], p_recv.at[k, off - 1], p_ss.at[k, off - 1], p_rs.at[k, off - 1], ty_peer(off))
            with scope(f"ssm_{strm}"):
                need(13 + lyr)
                step_sizes(k, lyr)
                state_update(k, lyr, strm)
            yield
            with scope(f"gate_{strm}"):
                z_in = (finish_sum(k, 1) * scale).astype(BF16).astype(F32)
                gated = ((yv_buf[k] + dsk_ref[lyr:lyr + 1, :] * xc_buf[k].astype(F32)) * (z_in * jax.nn.sigmoid(z_in))).astype(BF16)
                y_a[k, zi, yi] = gated[:, :half]
                y_b[k, zi, yi] = gated[:, half:]
            for off in range(1, n_y):
                push(y_a, k, zi, yi, ya_ss.at[k, off - 1], ya_rs.at[k, off - 1], at_y(off))
            for off in range(1, n_z):
                push(y_b, k, zi, yi, yb_ss.at[k, off - 1], yb_rs.at[k, off - 1], at_z(off))
            for out in range(1, n_z):
                push(y_a, k, zi, yi, ya2_ss.at[k, out - 1, 0], ya2_rs.at[k, out - 1, 0], at_z(out))
            for out in range(1, n_y):
                push(y_b, k, zi, yi, yb2_ss.at[k, out - 1, 0], yb2_rs.at[k, out - 1, 0], at_y(out))
            yield
            with scope(f"fwd_{strm}"):
                for off in range(1, max(n_y, n_z)):
                    if off < n_y:
                        landed(y_a, k, ya_ss.at[k, off - 1], ya_rs.at[k, off - 1])
                        for out in range(1, n_z):
                            push(y_a, k, zi, lax.rem(yi + n_y - off, n_y), ya2_ss.at[k, out - 1, off], ya2_rs.at[k, out - 1, off], at_z(out))
                    if off < n_z:
                        landed(y_b, k, yb_ss.at[k, off - 1], yb_rs.at[k, off - 1])
                        for out in range(1, n_y):
                            push(y_b, k, lax.rem(zi + n_z - off, n_z), yi, yb2_ss.at[k, out - 1, off], yb2_rs.at[k, out - 1, off], at_y(out))
            per_group = n_ty // n_z
            for off in range(n_z):
                if off < 2:
                    yield
                with scope(f"outmm_{strm}_{off}"):
                    zz = lax.rem(zi + n_z - off, n_z)
                    if off:
                        for oy in range(n_y):
                            landed(y_a, k, ya2_ss.at[k, off - 1, oy], ya2_rs.at[k, off - 1, oy])
                    for oy in range(1, n_y):
                        landed(y_b, k, yb2_ss.at[k, oy - 1, off], yb2_rs.at[k, oy - 1, off])
                    part = nn_dot(y_a[k, zz].reshape(group, half), wo_ref[lyr, :half]) + nn_dot(y_b[k, zz].reshape(group, half), wo_ref[lyr, half:])
                    for i in range(per_group):
                        o_send[k, zz * per_group + i] = part[i * own_rows:(i + 1) * own_rows].astype(BF16)
                    for i in range(per_group):
                        owner = zz * per_group + i
                        slot = lax.rem(owner - ty + n_ty - 1, n_ty)

                        @pl.when(owner != ty)
                        def _():
                            copy(o_send.at[k, owner], o_recv.at[k, slot], o_ss.at[k, slot], o_rs.at[k, slot], at_ty(owner)).start()

            yield
            with scope(f"wait_o_{strm}"):
                for off in range(1, n_ty):
                    await_recv(o_send.at[k, 0], o_recv.at[k, off - 1], o_ss.at[k, off - 1], o_rs.at[k, off - 1], at_ty(ty))
            sum_buf[k, ty] = add_up(o_send[k, ty], [o_recv[k, off - 1] for off in range(1, n_ty)]).astype(BF16)
            for off in range(1, n_ty):
                send(sum_buf.at[k, ty], sum_buf.at[k, ty], s_ss.at[k, off - 1], s_rs.at[k, off - 1], ty_peer(off))
            yield
            with scope(f"wait_s_{strm}"):
                for off in range(1, n_ty):
                    await_recv(sum_buf.at[k, 0], sum_buf.at[k, 0], s_ss.at[k, off - 1], s_rs.at[k, off - 1], at_ty(ty))
            target = res_out if lyr == layers - 1 else res_buf
            for blk in range(n_ty):
                span = slice(blk * own_blocks, (blk + 1) * own_blocks)
                total = source[span, strm] + sum_buf[k, blk].astype(F32).reshape(own_blocks, rows, LANES)
                target[span, strm] = total
            source = target

    moves = [(res_in, res_ref), (norm_in, norm_ref), (win_in, win_ref), (cw_in, cw_ref), (cb_in, cb_ref), (cs_in, cs_ref), (wx_in, wx_ref),
             (wdt_in, wdt_ref), (dtb_in, dtb_ref), (al_in, al_ref), (dsk_in, dsk_ref), (wo_in, wo_ref)]
    moves += [(ssm_in.at[lyr], ssm_buf.at[lyr]) for lyr in range(layers)]
    loads = [pltpu.make_async_copy(src, dst, in_sems.at[i]) for i, (src, dst) in enumerate(moves)]
    for load in loads:
        load.start()

    barrier = pltpu.get_barrier_semaphore()
    for off in range(1, n_y):
        pl.semaphore_signal(barrier, inc=1, device_id=at_y(off), device_id_type=MESH)
    for off in range(1, n_z):
        pl.semaphore_signal(barrier, inc=1, device_id=at_z(off), device_id_type=MESH)
    for off in range(1, n_ty):
        pl.semaphore_signal(barrier, inc=1, device_id=ty_peer(off), device_id_type=MESH)

    def need(count):
        while len(moves) - len(loads) < count:
            loads.pop(0).wait()

    need(3)
    for lyr in range(layers):
        for part in range(2):
            w_buf[lyr, part] = win_ref[lyr, :, part, :]
    streams = [stream(strm) for strm in range(n_str)]
    for strm in streams:
        next(strm)
    with scope("barrier"):
        pl.semaphore_wait(barrier, n_y + n_z + n_ty - 3)

    live = list(streams)
    turn = 0
    while live:
        for idx, strm in enumerate(streams):
            if strm in live and turn >= idx * lag:
                try:
                    next(strm)
                except StopIteration:
                    live.remove(strm)
        turn += 1

    with scope("drain"):
        for desc in pending:
            desc.wait_send()
        for k in range(layers * n_str):
            for off in range(1, n_ty):
                copy(o_send.at[k, 0], o_recv.at[k, off - 1], o_ss.at[k, off - 1], o_rs.at[k, off - 1], at_ty(ty)).wait_send()


def store_kernel(res_ref, conv_ref, ssm_ref, res_out, conv_out, ssm_out, sems):
    copies = [pltpu.make_async_copy(src, dst, sems.at[i]) for i, (src, dst) in enumerate([(ssm_ref, ssm_out), (res_ref, res_out), (conv_ref, conv_out)])]
    for desc in copies:
        desc.start()
    for desc in copies:
        desc.wait()


def on_chip(shape, dtype):
    return pltpu.VMEM(shape, dtype)


def from_chip(array):
    return pltpu.with_memory_space_constraint(array, pltpu.VMEM)


def build(mesh, n_y, n_str, lag):
    n_tx, n_ty = mesh.shape["tx"], mesh.shape["ty"]
    n_z = n_tx // n_y

    def local_step(residual, norm_w, w_in, conv_w, conv_b, w_x, w_dt, dt_bias, a_log, d_skip, w_out, conv_state, ssm_state):
        layers, batch, chans, n_state = ssm_state.shape
        rows = batch // n_str
        all_rows, d_local = residual.shape
        rank = w_dt.shape[1]
        half = chans // 2
        own = all_rows // n_ty // n_str
        pk = rows * 2 * n_state // LANES
        ks = layers * n_str
        dims = (n_z, n_y, n_ty, n_str, rows, layers, d_local * n_tx, n_state, rank, lag)
        vmem = pl.BlockSpec(memory_space=pltpu.VMEM)
        anyspace = pl.BlockSpec(memory_space=pl.ANY)
        dma = pltpu.SemaphoreType.DMA
        res_shape = (n_tx, n_str, rows, d_local)
        conv_shape = (layers, 3, batch, chans)
        ssm_shape = (layers, batch, n_state, chans)
        operands = [
            residual.reshape(res_shape), norm_w, w_in, conv_w.transpose(0, 2, 1), conv_b, w_x.transpose(0, 2, 1), w_dt, dt_bias,
            a_log.transpose(0, 2, 1), d_skip, w_out, conv_state.transpose(0, 3, 1, 2), ssm_state.transpose(0, 1, 3, 2),
        ]
        scratch = [pltpu.VMEM(op.shape, op.dtype) for op in operands[:-1]]
        scratch += [
            pltpu.VMEM((layers, 2, d_local, chans), BF16),
            pltpu.VMEM((ks, 2, n_y, n_z * rows, half), BF16),
            pltpu.VMEM((ks, 2, n_y - 1, n_z * rows, half), BF16),
            pltpu.VMEM((ks, 2, n_z, n_y * rows, half), BF16),
            pltpu.VMEM((ks, 2, n_z - 1, n_y * rows, half), BF16),
            pltpu.VMEM((ks, 2, n_z, rows, half), BF16),
            pltpu.VMEM((ks, 2, n_z - 1, rows, half), BF16),
            pltpu.VMEM((ks, 2, n_y, rows, half), BF16),
            pltpu.VMEM((ks, 2, n_y - 1, rows, half), BF16),
            pltpu.VMEM((ks, n_z, 8, n_y * rows), F32),
            pltpu.VMEM((ks, n_z - 1, 8, n_y * rows), F32),
            pltpu.VMEM((ks, 8, n_y * rows), F32),
            pltpu.VMEM((ks, n_y - 1, 8, n_y * rows), F32),
            pltpu.VMEM((ks, n_y * rows, 8), F32),
            pltpu.VMEM((ks, rows + pk, LANES), BF16),
            pltpu.VMEM((ks, n_ty - 1, rows + pk, LANES), BF16),
            pltpu.VMEM((ks, n_z, n_y, rows, half), BF16),
            pltpu.VMEM((ks, n_z, n_y, rows, half), BF16),
            pltpu.VMEM((ks, n_ty, own, d_local), BF16),
            pltpu.VMEM((ks, n_ty - 1, own, d_local), BF16),
            pltpu.VMEM((ks, n_ty, own, d_local), BF16),
            pltpu.VMEM(res_shape, F32),
            pltpu.VMEM((ks, rows, chans), F32),
            pltpu.VMEM((ks, rows, chans), F32),
            pltpu.VMEM((ks, rows, LANES), F32),
            pltpu.VMEM((ks, rows, chans), F32),
            pltpu.VMEM((ks, rows, chans), BF16),
        ]
        y1, z1, t1 = n_y - 1, n_z - 1, n_ty - 1
        for shape in [(ks, 2, y1), (ks, 2, z1), (ks, 2, z1), (ks, 2, y1), (ks, z1), (ks, y1), (ks, t1),
                      (ks, y1), (ks, z1), (ks, z1, n_y), (ks, y1, n_z), (ks, t1), (ks, t1)]:
            scratch += [dma(shape), dma(shape)]
        scratch += [dma((len(operands) - 1 + layers,))]
        res, conv, ssm = pl.pallas_call(
            functools.partial(step_kernel, dims),
            out_shape=(on_chip(res_shape, F32), on_chip(conv_shape, BF16), on_chip(ssm_shape, F32)),
            in_specs=[pl.BlockSpec(memory_space=pltpu.HBM)] * len(operands),
            out_specs=(vmem, vmem, vmem),
            scratch_shapes=scratch,
            compiler_params=pltpu.CompilerParams(collective_id=0, has_side_effects=True, vmem_limit_bytes=VMEM_LIMIT),
        )(*operands)
        res, conv, ssm = pl.pallas_call(
            store_kernel,
            out_shape=(jax.ShapeDtypeStruct(res_shape, F32), jax.ShapeDtypeStruct(conv_shape, BF16), jax.ShapeDtypeStruct(ssm_shape, F32)),
            in_specs=[vmem] * 3,
            out_specs=(anyspace,) * 3,
            scratch_shapes=[dma((3,))],
            compiler_params=pltpu.CompilerParams(vmem_limit_bytes=16 * 1024 * 1024),
        )(*(from_chip(out) for out in (res, conv, ssm)))
        return res.reshape(all_rows, d_local), conv.transpose(0, 2, 3, 1), ssm.transpose(0, 1, 3, 2)

    cache_spec = P(None, ("dp", "tx"), "ty", None)
    in_specs = (P("dp", "tx"), P(None, "tx"), P(None, "tx", None, "ty"), P(None, "ty", None), P(None, "ty"), P(None, "ty", None), P(None, None, "ty"), P(None, "ty"), P(None, "ty", None), P(None, "ty"), P(None, "ty", "tx"), cache_spec, cache_spec)
    out_specs = (P("dp", "tx"), cache_spec, cache_spec)
    return jax.shard_map(local_step, mesh=mesh, in_specs=in_specs, out_specs=out_specs, check_vma=False)


def solution(mesh):
    return build(mesh, 4, 2, 1)
```

time: 512 us -> 99.6 us (0.19)
  waiting for transfers between devices: 347 us -> 0 us
  blocking collectives: 115 us -> 0 us
  Pallas kernels: 0 us -> 98.8 us
  other arithmetic: 17.6 us -> 0 us
  between operations: 14.5 us -> 0.64 us
  matrix products: 11.9 us -> 0 us
    reduce_scatter x2 -> x0, waiting for transfers between devices: 153 us -> none  [local_step(): lax.psum_scatter(proj_part.astype(jnp.bfloat16), 'tx', scatter_dimension=...]
    psum x2 -> x0, waiting for transfers between devices: 118 us -> none  [sum_over_ty(): return lax.psum(part_sum.astype(jnp.bfloat16), 'ty').astype(jnp.float32)]
    psum x4 -> x0, blocking collectives: 115 us -> none  [the longest x2 69.3 us: local_step(): sq_total = lax.psum(sq_part, 'tx')]
    pallas_call x0 -> x2, Pallas kernels: none -> 98.8 us  [the longest x1 96.5 us: local_step(): pl.pallas_call(functools.partial(step_kernel, dims), out_shape=(on_chip(r...]
    all_gather x2 -> x0, waiting for transfers between devices: 75.1 us -> none  [local_step(): gated_rows = lax.all_gather(gated, 'tx', axis=0, tiled=True)]
    dot_general x8 -> x0, matrix products: 11.9 us -> none  [the longest x2 6.21 us: local_step(): jnp.einsum('bd,dke->bke', normed, w_in[layer_idx], preferred_element_type...]
    reduce_sum x10 -> x0, other arithmetic: 8.04 us -> none  [the longest x2 4.96 us: channel_update(): state_val = jnp.sum(ssm_new * c_mat[:, None, :], axis=-1)]
  transfers between devices with their start and end apart: 6 -> 0, of which waited for: 6 -> 0; matrix products, arithmetic and copies ran while one was open for 1% -> 0% of each run, Pallas kernels for 0% -> 0%
where the time goes in v2:
time: 99.6 us; the launch traced here: 99.5 us
  Pallas kernels  98.8 us (99%)
    pallas_call x1, Pallas kernels, local_step(): pl.pallas_call(functools.partial(step_kernel, dims), out_shape=(on_chip(r...  96.5 us
    pallas_call x1, Pallas kernels, local_step(): pl.pallas_call(store_kernel, out_shape=(jax.ShapeDtypeStruct(res_shape, F...  2.31 us

profile of v2, /device:TPU:1, one launch (start us, length us, event | category | flops | bytes accessed | tf_op | source)
XLA Modules:
  0.0 99.5 jit_solution(3682151334269593814)
XLA Ops:
  0.6 96.5 %shard_map.148 = (f32[16,2,32,128]{3,2,1,0:T(8,128)S(1)}, bf16[2,3,64,512]{3,2,1,0:T(8,128)(2,1)S(1)}, f32[2,64,16,512]{3,2,1,0:T(8,128)S(1)}) custom-call(f32[16,2,32,128]{3,2,1,0:T(8,128)} %bitcast.10, f32[2,128]{1,0:T(2,128)} %norm_in.1, bf16[2,128,2,512]{3,2,1,0:T(2,128)(2,1)} %win_in.1, f32[2,4,512]{2,1,0:T(4,128)} %bitcast.14, f32[2,512]{1,0:T(2,128)} %cb_in.1, ...), custom_call_target="tpu_custom_call" | custom-call | tf_op jit(solution)/shard_map/pallas_call | solution.py:430
  97.2 2.3 %shard_map.149 = (f32[16,2,32,128]{3,2,1,0:T(8,128)}, bf16[2,3,64,512]{3,2,1,0:T(8,128)(2,1)}, f32[2,64,16,512]{3,2,1,0:T(8,128)}) custom-call(f32[16,2,32,128]{3,2,1,0:T(8,128)S(1)} %get-tuple-element.9.res_ref, bf16[2,3,64,512]{3,2,1,0:T(8,128)(2,1)S(1)} %get-tuple-element.10.conv_ref, f32[2,64,16,512]{3,2,1,0:T(8,128)S(1)} %get-tuple-element.11.ssm_ref), custom_call_target="tpu_custom_call" | custom-call | tf_op jit(solution)/shard_map/pallas_call | solution.py:438

commit v3 on v2

--- a/solution.py
+++ b/solution.py
@@ -13,6 +13,14 @@
 F32 = jnp.float32
 BF16 = jnp.bfloat16
 LANES = 128
+GATE = 10
+STREAMS = 4
+ORDER = (
+    1, 0, 11, 1, 10, 0, 2, 11, 1, 12, 3, 0, 10, 2, 1, 1, 0, 13, 3, 0, 2, 12, 1, 13,
+    3, 0, 2, 2, 1, 3, 3, 2, 0, 1, 3, 0, 2, 1, 11, 3, 0, 2, 10, 1, 3, 2, 11, 0,
+    3, 12, 1, 2, 13, 1, 3, 1, 10, 0, 12, 2, 13, 3, 1, 0, 0, 2, 2, 3, 3, 0, 2, 3,
+    1, 0, 2, 3, 1, 0, 2, 3, 0, 1, 2, 3,
+)
 VMEM_LIMIT = 52 * 1024 * 1024
 
 
@@ -33,9 +41,9 @@
                 res_ref, norm_ref, win_ref, cw_ref, cb_ref, wx_ref, wdt_ref, dtb_ref, al_ref, dsk_ref, wo_ref, cs_ref,
                 w_buf, send_a, recv_a, send_b, recv_b, send_a2, recv_a2, send_b2, recv_b2, st_send, st_recv, st2_send, st2_recv, stat_t,
                 p_send, p_recv, y_a, y_b, o_send, o_recv, sum_buf, res_buf, dt_buf, dx_buf, bc_buf, yv_buf, xc_buf,
-                a_ss, a_rs, b_ss, b_rs, a2_ss, a2_rs, b2_ss, b2_rs, st_ss, st_rs, st2_ss, st2_rs, p_ss, p_rs,
-                ya_ss, ya_rs, yb_ss, yb_rs, ya2_ss, ya2_rs, yb2_ss, yb2_rs, o_ss, o_rs, s_ss, s_rs, in_sems):
-    n_z, n_y, n_ty, n_str, rows, layers, d_model, n_state, rank, lag = dims
+                in_sems, *sem_refs):
+    m_a, m_b, m_a2, m_b2, m_st, m_st2, m_p, m_ya, m_yb, m_ya2, m_yb2, m_o, m_s = [(sem_refs[2 * i], sem_refs[2 * i + 1]) for i in range(len(sem_refs) // 2)]
+    n_z, n_y, n_ty, n_str, rows, layers, d_model, n_state, rank, order = dims
     tx, ty = lax.axis_index("tx"), lax.axis_index("ty")
     zi, yi = tx // n_y, tx % n_y
     chans = win_ref.shape[-1]
@@ -44,6 +52,7 @@
     own_rows = own_blocks * rows
     group = n_y * rows
     pk = p_send.shape[1] - rows
+    y1, z1, t1 = n_y - 1, n_z - 1, n_ty - 1
     scope = jax.named_scope
 
     def y_peer(off):
@@ -64,23 +73,27 @@
     def ty_peer(off):
         return at_ty(lax.rem(ty + off, n_ty))
 
-    pending = []
-
-    def copy(src, dst, ssem, rsem, device):
-        return pltpu.make_async_remote_copy(src_ref=src, dst_ref=dst, send_sem=ssem, recv_sem=rsem, device_id=device, device_id_type=MESH)
-
-    def send(src, dst, ssem, rsem, device):
-        desc = copy(src, dst, ssem, rsem, device)
-        desc.start()
-        pending.append(desc)
-
-    def await_recv(src, dst, ssem, rsem, device):
-        copy(src, dst, ssem, rsem, device).wait_recv()
+    def send(src, dst, sems, slot, device):
+        pltpu.make_async_remote_copy(src_ref=src, dst_ref=dst, send_sem=sems[0], recv_sem=sems[1].at[slot], device_id=device, device_id_type=MESH).start()
+
+    def arrived(ref, sems, slot):
+        pltpu.make_async_remote_copy(src_ref=ref, dst_ref=ref, send_sem=sems[0], recv_sem=sems[1].at[slot], device_id=ty_peer(1), device_id_type=MESH).wait_recv()
+
+    def departed(ref, sems):
+        pltpu.make_async_remote_copy(src_ref=ref, dst_ref=ref, send_sem=sems[0], recv_sem=sems[1].at[0], device_id=ty_peer(1), device_id_type=MESH).wait_send()
 
     def add_up(first, others):
         return functools.reduce(jnp.add, [o.astype(F32) for o in others], first.astype(F32))
 
+    split = set()
+
+    def split_weight(lyr, part):
+        if (lyr, part) not in split:
+            split.add((lyr, part))
+            w_buf[lyr, part] = win_ref[lyr, :, part, :]
+
     def input_matmul(k, lyr, strm, source, part):
+        split_weight(lyr, part)
         norm = norm_ref[lyr:lyr + 1, :]
         for zz in range(n_z):
             res = source[zz * n_y:(zz + 1) * n_y, strm].reshape(group, LANES)
@@ -94,50 +107,44 @@
     def phase_one(k, part):
         for off in range(1, n_z):
             if part == 0:
-                send(st_send.at[k, z_peer(off)], st_recv.at[k, off - 1], st_ss.at[k, off - 1], st_rs.at[k, off - 1], at_z(off))
+                send(st_send.at[k, z_peer(off)], st_recv.at[k, off - 1], m_st, k, at_z(off))
         for off in range(1, max(n_y, n_z)):
             if off < n_y:
-                send(send_a.at[k, part, y_peer(off)], recv_a.at[k, part, off - 1], a_ss.at[k, part, off - 1], a_rs.at[k, part, off - 1], at_y(off))
+                send(send_a.at[k, part, y_peer(off)], recv_a.at[k, part, off - 1], m_a, 2 * k + part, at_y(off))
             if off < n_z:
-                send(send_b.at[k, part, z_peer(off)], recv_b.at[k, part, off - 1], b_ss.at[k, part, off - 1], b_rs.at[k, part, off - 1], at_z(off))
+                send(send_b.at[k, part, z_peer(off)], recv_b.at[k, part, off - 1], m_b, 2 * k + part, at_z(off))
 
     def phase_two(k, part):
         if part == 0:
-            for off in range(1, n_z):
-                await_recv(st_send.at[k, 0], st_recv.at[k, off - 1], st_ss.at[k, off - 1], st_rs.at[k, off - 1], at_z(off))
+            arrived(st_recv.at[k], m_st, k)
             st2_send[k] = add_up(st_send[k, zi], [st_recv[k, off - 1] for off in range(1, n_z)])
             for off in range(1, n_y):
-                send(st2_send.at[k], st2_recv.at[k, off - 1], st2_ss.at[k, off - 1], st2_rs.at[k, off - 1], at_y(off))
+                send(st2_send.at[k], st2_recv.at[k, off - 1], m_st2, k, at_y(off))
         with scope(f"wait_a1_{part}"):
-            for off in range(1, n_y):
-                await_recv(send_a.at[k, part, 0], recv_a.at[k, part, off - 1], a_ss.at[k, part, off - 1], a_rs.at[k, part, off - 1], at_y(off))
+            arrived(recv_a.at[k, part], m_a, 2 * k + part)
         for zz in range(n_z):
             span = slice(zz * rows, (zz + 1) * rows)
             send_a2[k, part, zz] = add_up(send_a[k, part, yi, span, :], [recv_a[k, part, off - 1, span, :] for off in range(1, n_y)]).astype(BF16)
         for off in range(1, n_z):
-            send(send_a2.at[k, part, z_peer(off)], recv_a2.at[k, part, off - 1], a2_ss.at[k, part, off - 1], a2_rs.at[k, part, off - 1], at_z(off))
+            send(send_a2.at[k, part, z_peer(off)], recv_a2.at[k, part, off - 1], m_a2, 2 * k + part, at_z(off))
         with scope(f"wait_b1_{part}"):
-            for off in range(1, n_z):
-                await_recv(send_b.at[k, part, 0], recv_b.at[k, part, off - 1], b_ss.at[k, part, off - 1], b_rs.at[k, part, off - 1], at_z(off))
+            arrived(recv_b.at[k, part], m_b, 2 * k + part)
         for yy in range(n_y):
             span = slice(yy * rows, (yy + 1) * rows)
             send_b2[k, part, yy] = add_up(send_b[k, part, zi, span, :], [recv_b[k, part, off - 1, span, :] for off in range(1, n_z)]).astype(BF16)
         for off in range(1, n_y):
-            send(send_b2.at[k, part, y_peer(off)], recv_b2.at[k, part, off - 1], b2_ss.at[k, part, off - 1], b2_rs.at[k, part, off - 1], at_y(off))
+            send(send_b2.at[k, part, y_peer(off)], recv_b2.at[k, part, off - 1], m_b2, 2 * k + part, at_y(off))
 
     def finish_sum(k, part):
         with scope(f"wait_2_{part}"):
-            for off in range(1, n_z):
-                await_recv(send_a2.at[k, part, 0], recv_a2.at[k, part, off - 1], a2_ss.at[k, part, off - 1], a2_rs.at[k, part, off - 1], at_z(off))
-            for off in range(1, n_y):
-                await_recv(send_b2.at[k, part, 0], recv_b2.at[k, part, off - 1], b2_ss.at[k, part, off - 1], b2_rs.at[k, part, off - 1], at_y(off))
+            arrived(recv_a2.at[k, part], m_a2, 2 * k + part)
+            arrived(recv_b2.at[k, part], m_b2, 2 * k + part)
         tot_a = add_up(send_a2[k, part, zi], [recv_a2[k, part, off - 1] for off in range(1, n_z)])
         tot_b = add_up(send_b2[k, part, yi], [recv_b2[k, part, off - 1] for off in range(1, n_y)])
         return jnp.concatenate([tot_a, tot_b], axis=-1)
 
     def row_scale(k):
-        for off in range(1, n_y):
-            await_recv(st2_send.at[k], st2_recv.at[k, off - 1], st2_ss.at[k, off - 1], st2_rs.at[k, off - 1], at_y(off))
+        arrived(st2_recv.at[k], m_st2, k)
         stat_t[k] = add_up(st2_send[k], [st2_recv[k, off - 1] for off in range(1, n_y)]).T
         mine = stat_t[k, pl.ds(pl.multiple_of(yi * rows, 8), rows), :][:, :1]
         return lax.rsqrt(mine / d_model + NORM_EPS)
@@ -198,43 +205,36 @@
 
         lax.fori_loop(0, rows // 8, update, 0)
 
-    def push(buf, k, zz, yy, ssem, rsem, device):
-        send(buf.at[k, zz, yy], buf.at[k, zz, yy], ssem, rsem, device)
-
-    def landed(buf, k, ssem, rsem):
-        await_recv(buf.at[k, 0, 0], buf.at[k, 0, 0], ssem, rsem, at_ty(ty))
-
-    def stream(strm):
+    def push(buf, k, zz, yy, sems, slot, device):
+        send(buf.at[k, zz, yy], buf.at[k, zz, yy], sems, slot, device)
+
+    def main_thread(strm):
         mine = slice(strm * rows, (strm + 1) * rows)
         source = res_ref
         for lyr in range(layers):
             k = lyr * n_str + strm
-            with scope(f"matmul_{strm}"):
-                input_matmul(k, lyr, strm, source, 0)
-            if lyr == 0:
-                input_matmul(k, lyr, strm, source, 1)
-                yield
+            if lyr:
+                source = gather_sums(k - n_str, lyr - 1, strm, source)
+                with scope(f"matmul_{strm}"):
+                    input_matmul(k, lyr, strm, source, 0)
+            elif strm != order[0]:
+                with scope(f"matmul_{strm}"):
+                    input_matmul(k, lyr, strm, source, 0)
+            sources[k] = source
             phase_one(k, 0)
-            if lyr:
-                input_matmul(k, lyr, strm, source, 1)
             yield
             with scope(f"phase2_{strm}"):
                 phase_two(k, 0)
-            phase_one(k, 1)
             yield
             with scope(f"xconv_{strm}"):
                 scale = row_scale(k)
                 need(7)
                 conv_and_proj(k, lyr, mine, (finish_sum(k, 0) * scale).astype(BF16))
             for off in range(1, n_ty):
-                send(p_send.at[k], p_recv.at[k, off - 1], p_ss.at[k, off - 1], p_rs.at[k, off - 1], ty_peer(off))
-            yield
-            with scope(f"phase2z_{strm}"):
-                phase_two(k, 1)
+                send(p_send.at[k], p_recv.at[k, off - 1], m_p, k, ty_peer(off))
             yield
             with scope(f"wait_p_{strm}"):
-                for off in range(1, n_ty):
-                    await_recv(p_send.at[k], p_recv.at[k, off - 1], p_ss.at[k, off - 1], p_rs.at[k, off - 1], ty_peer(off))
+                arrived(p_recv.at[k], m_p, k)
             with scope(f"ssm_{strm}"):
                 need(13 + lyr)
                 step_sizes(k, lyr)
@@ -246,35 +246,32 @@
                 y_a[k, zi, yi] = gated[:, :half]
                 y_b[k, zi, yi] = gated[:, half:]
             for off in range(1, n_y):
-                push(y_a, k, zi, yi, ya_ss.at[k, off - 1], ya_rs.at[k, off - 1], at_y(off))
+                push(y_a, k, zi, yi, m_ya, k * y1 + off - 1, at_y(off))
             for off in range(1, n_z):
-                push(y_b, k, zi, yi, yb_ss.at[k, off - 1], yb_rs.at[k, off - 1], at_z(off))
+                push(y_b, k, zi, yi, m_yb, k * z1 + off - 1, at_z(off))
             for out in range(1, n_z):
-                push(y_a, k, zi, yi, ya2_ss.at[k, out - 1, 0], ya2_rs.at[k, out - 1, 0], at_z(out))
+                push(y_a, k, zi, yi, m_ya2, k * z1 + out - 1, at_z(out))
             for out in range(1, n_y):
-                push(y_b, k, zi, yi, yb2_ss.at[k, out - 1, 0], yb2_rs.at[k, out - 1, 0], at_y(out))
+                push(y_b, k, zi, yi, m_yb2, k * n_z, at_y(out))
             yield
             with scope(f"fwd_{strm}"):
                 for off in range(1, max(n_y, n_z)):
                     if off < n_y:
-                        landed(y_a, k, ya_ss.at[k, off - 1], ya_rs.at[k, off - 1])
+                        arrived(y_a.at[k, 0, 0], m_ya, k * y1 + off - 1)
                         for out in range(1, n_z):
-                            push(y_a, k, zi, lax.rem(yi + n_y - off, n_y), ya2_ss.at[k, out - 1, off], ya2_rs.at[k, out - 1, off], at_z(out))
+                            push(y_a, k, zi, lax.rem(yi + n_y - off, n_y), m_ya2, k * z1 + out - 1, at_z(out))
                     if off < n_z:
-                        landed(y_b, k, yb_ss.at[k, off - 1], yb_rs.at[k, off - 1])
+                        arrived(y_b.at[k, 0, 0], m_yb, k * z1 + off - 1)
                         for out in range(1, n_y):
-                            push(y_b, k, lax.rem(zi + n_z - off, n_z), yi, yb2_ss.at[k, out - 1, off], yb2_rs.at[k, out - 1, off], at_y(out))
+                            push(y_b, k, lax.rem(zi + n_z - off, n_z), yi, m_yb2, k * n_z + off, at_y(out))
+            yield
             per_group = n_ty // n_z
             for off in range(n_z):
-                if off < 2:
-                    yield
                 with scope(f"outmm_{strm}_{off}"):
                     zz = lax.rem(zi + n_z - off, n_z)
                     if off:
-                        for oy in range(n_y):
-                            landed(y_a, k, ya2_ss.at[k, off - 1, oy], ya2_rs.at[k, off - 1, oy])
-                    for oy in range(1, n_y):
-                        landed(y_b, k, yb2_ss.at[k, oy - 1, off], yb2_rs.at[k, oy - 1, off])
+                        arrived(y_a.at[k, 0], m_ya2, k * z1 + off - 1)
+                    arrived(y_b.at[k, 0, :y1], m_yb2, k * n_z + off)
                     part = nn_dot(y_a[k, zz].reshape(group, half), wo_ref[lyr, :half]) + nn_dot(y_b[k, zz].reshape(group, half), wo_ref[lyr, half:])
                     for i in range(per_group):
                         o_send[k, zz * per_group + i] = part[i * own_rows:(i + 1) * own_rows].astype(BF16)
@@ -284,31 +281,43 @@
 
                         @pl.when(owner != ty)
                         def _():
-                            copy(o_send.at[k, owner], o_recv.at[k, slot], o_ss.at[k, slot], o_rs.at[k, slot], at_ty(owner)).start()
+                            send(o_send.at[k, owner], o_recv.at[k, slot], m_o, k, at_ty(owner))
 
             yield
             with scope(f"wait_o_{strm}"):
-                for off in range(1, n_ty):
-                    await_recv(o_send.at[k, 0], o_recv.at[k, off - 1], o_ss.at[k, off - 1], o_rs.at[k, off - 1], at_ty(ty))
+                arrived(o_recv.at[k], m_o, k)
             sum_buf[k, ty] = add_up(o_send[k, ty], [o_recv[k, off - 1] for off in range(1, n_ty)]).astype(BF16)
             for off in range(1, n_ty):
-                send(sum_buf.at[k, ty], sum_buf.at[k, ty], s_ss.at[k, off - 1], s_rs.at[k, off - 1], ty_peer(off))
-            yield
-            with scope(f"wait_s_{strm}"):
-                for off in range(1, n_ty):
-                    await_recv(sum_buf.at[k, 0], sum_buf.at[k, 0], s_ss.at[k, off - 1], s_rs.at[k, off - 1], at_ty(ty))
-            target = res_out if lyr == layers - 1 else res_buf
-            for blk in range(n_ty):
-                span = slice(blk * own_blocks, (blk + 1) * own_blocks)
-                total = source[span, strm] + sum_buf[k, blk].astype(F32).reshape(own_blocks, rows, LANES)
-                target[span, strm] = total
-            source = target
-
+                send(sum_buf.at[k, ty], sum_buf.at[k, ty], m_s, k, ty_peer(off))
+            yield
+        gather_sums(k, lyr, strm, source)
+
+    def gather_sums(k, lyr, strm, source):
+        with scope(f"wait_s_{strm}"):
+            arrived(sum_buf.at[k, :t1], m_s, k)
+        target = res_out if lyr == layers - 1 else res_buf
+        for blk in range(n_ty):
+            span = slice(blk * own_blocks, (blk + 1) * own_blocks)
+            target[span, strm] = source[span, strm] + sum_buf[k, blk].astype(F32).reshape(own_blocks, rows, LANES)
+        return target
+
+    def gate_thread(strm):
+        for lyr in range(layers):
+            k = lyr * n_str + strm
+            with scope(f"matmulz_{strm}"):
+                input_matmul(k, lyr, strm, sources[k], 1)
+            phase_one(k, 1)
+            yield
+            with scope(f"phase2z_{strm}"):
+                phase_two(k, 1)
+            yield
+
+    sources = {}
     moves = [(res_in, res_ref), (norm_in, norm_ref), (win_in, win_ref), (cw_in, cw_ref), (cb_in, cb_ref), (cs_in, cs_ref), (wx_in, wx_ref),
              (wdt_in, wdt_ref), (dtb_in, dtb_ref), (al_in, al_ref), (dsk_in, dsk_ref), (wo_in, wo_ref)]
     moves += [(ssm_in.at[lyr], ssm_buf.at[lyr]) for lyr in range(layers)]
     loads = [pltpu.make_async_copy(src, dst, in_sems.at[i]) for i, (src, dst) in enumerate(moves)]
-    for load in loads:
+    for load in loads[:3]:
         load.start()
 
     barrier = pltpu.get_barrier_semaphore()
@@ -324,32 +333,25 @@
             loads.pop(0).wait()
 
     need(3)
-    for lyr in range(layers):
-        for part in range(2):
-            w_buf[lyr, part] = win_ref[lyr, :, part, :]
-    streams = [stream(strm) for strm in range(n_str)]
-    for strm in streams:
-        next(strm)
+    for load in loads:
+        load.start()
+    with scope("matmul_first"):
+        input_matmul(order[0], 0, order[0], res_ref, 0)
     with scope("barrier"):
         pl.semaphore_wait(barrier, n_y + n_z + n_ty - 3)
 
-    live = list(streams)
-    turn = 0
-    while live:
-        for idx, strm in enumerate(streams):
-            if strm in live and turn >= idx * lag:
-                try:
-                    next(strm)
-                except StopIteration:
-                    live.remove(strm)
-        turn += 1
+    threads = {}
+    for strm in range(n_str):
+        threads[strm] = main_thread(strm)
+        threads[GATE + strm] = gate_thread(strm)
+    for name in order:
+        next(threads[name], None)
 
     with scope("drain"):
-        for desc in pending:
-            desc.wait_send()
-        for k in range(layers * n_str):
-            for off in range(1, n_ty):
-                copy(o_send.at[k, 0], o_recv.at[k, off - 1], o_ss.at[k, off - 1], o_rs.at[k, off - 1], at_ty(ty)).wait_send()
+        sent = [recv_a, recv_b, recv_a2, recv_b2, st_recv, st2_recv, p_recv, y_a.at[:, 0, :y1], y_b.at[:, 0, :z1],
+                y_a.at[:, :z1], y_b.at[:, :, :y1], o_recv, sum_buf.at[:, :t1]]
+        for ref, sems in zip(sent, [m_a, m_b, m_a2, m_b2, m_st, m_st2, m_p, m_ya, m_yb, m_ya2, m_yb2, m_o, m_s]):
+            departed(ref, sems)
 
 
 def store_kernel(res_ref, conv_ref, ssm_ref, res_out, conv_out, ssm_out, sems):
@@ -368,7 +370,7 @@
     return pltpu.with_memory_space_constraint(array, pltpu.VMEM)
 
 
-def build(mesh, n_y, n_str, lag):
+def build(mesh, n_y, n_str, order):
     n_tx, n_ty = mesh.shape["tx"], mesh.shape["ty"]
     n_z = n_tx // n_y
 
@@ -381,7 +383,7 @@
         own = all_rows // n_ty // n_str
         pk = rows * 2 * n_state // LANES
         ks = layers * n_str
-        dims = (n_z, n_y, n_ty, n_str, rows, layers, d_local * n_tx, n_state, rank, lag)
+        dims = (n_z, n_y, n_ty, n_str, rows, layers, d_local * n_tx, n_state, rank, order)
         vmem = pl.BlockSpec(memory_space=pltpu.VMEM)
         anyspace = pl.BlockSpec(memory_space=pl.ANY)
         dma = pltpu.SemaphoreType.DMA
@@ -423,10 +425,9 @@
             pltpu.VMEM((ks, rows, chans), BF16),
         ]
         y1, z1, t1 = n_y - 1, n_z - 1, n_ty - 1
-        for shape in [(ks, 2, y1), (ks, 2, z1), (ks, 2, z1), (ks, 2, y1), (ks, z1), (ks, y1), (ks, t1),
-                      (ks, y1), (ks, z1), (ks, z1, n_y), (ks, y1, n_z), (ks, t1), (ks, t1)]:
-            scratch += [dma(shape), dma(shape)]
         scratch += [dma((len(operands) - 1 + layers,))]
+        for count in [2 * ks, 2 * ks, 2 * ks, 2 * ks, ks, ks, ks, ks * y1, ks * z1, ks * z1, ks * n_z, ks, ks]:
+            scratch += [dma, dma((count,))]
         res, conv, ssm = pl.pallas_call(
             functools.partial(step_kernel, dims),
             out_shape=(on_chip(res_shape, F32), on_chip(conv_shape, BF16), on_chip(ssm_shape, F32)),
@@ -452,4 +453,4 @@
 
 
 def solution(mesh):
-    return build(mesh, 4, 2, 1)
+    return build(mesh, 4, STREAMS, ORDER)

time: 99.6 us -> 80.7 us (0.81)
  Pallas kernels: 98.8 us -> 79.9 us
    pallas_call x1, Pallas kernels: 96.5 us -> 77.6 us  [local_step(): pl.pallas_call(functools.partial(step_kernel, dims), out_shape=(on_chip(r...]
where the time goes in v3:
time: 80.7 us; the launch traced here: 80.6 us
  Pallas kernels  79.9 us (99%)
    pallas_call x1, Pallas kernels, local_step(): pl.pallas_call(functools.partial(step_kernel, dims), out_shape=(on_chip(r...  77.6 us
    pallas_call x1, Pallas kernels, local_step(): pl.pallas_call(store_kernel, out_shape=(jax.ShapeDtypeStruct(res_shape, F...  2.31 us

profile of v3, /device:TPU:1, one launch (start us, length us, event | category | flops | bytes accessed | tf_op | source)
XLA Modules:
  0.0 80.6 jit_solution(12822131258755234039)
XLA Ops:
  0.6 77.6 %shard_map.148 = (f32[16,4,16,128]{3,2,1,0:T(8,128)S(1)}, bf16[2,3,64,512]{3,2,1,0:T(8,128)(2,1)S(1)}, f32[2,64,16,512]{3,2,1,0:T(8,128)S(1)}) custom-call(f32[16,4,16,128]{3,2,1,0:T(8,128)} %bitcast.10, f32[2,128]{1,0:T(2,128)} %norm_in.1, bf16[2,128,2,512]{3,2,1,0:T(2,128)(2,1)} %win_in.1, f32[2,4,512]{2,1,0:T(4,128)} %bitcast.14, f32[2,512]{1,0:T(2,128)} %cb_in.1, ...), custom_call_target="tpu_custom_call" | custom-call | tf_op jit(solution)/shard_map/pallas_call | solution.py:431
  78.3 2.3 %shard_map.149 = (f32[16,4,16,128]{3,2,1,0:T(8,128)}, bf16[2,3,64,512]{3,2,1,0:T(8,128)(2,1)}, f32[2,64,16,512]{3,2,1,0:T(8,128)}) custom-call(f32[16,4,16,128]{3,2,1,0:T(8,128)S(1)} %get-tuple-element.9.res_ref, bf16[2,3,64,512]{3,2,1,0:T(8,128)(2,1)S(1)} %get-tuple-element.10.conv_ref, f32[2,64,16,512]{3,2,1,0:T(8,128)S(1)} %get-tuple-element.11.ssm_ref), custom_call_target="tpu_custom_call" | custom-call | tf_op jit(solution)/shard_map/pallas_call | solution.py:439

commit v4 on v3

--- a/solution.py
+++ b/solution.py
@@ -14,12 +14,16 @@
 BF16 = jnp.bfloat16
 LANES = 128
 GATE = 10
+WEIGHT = 20
+W_IN = 30
+PIECES = 4
+CUT = 2
 STREAMS = 4
 ORDER = (
-    1, 0, 11, 1, 10, 0, 2, 11, 1, 12, 3, 0, 10, 2, 1, 1, 0, 13, 3, 0, 2, 12, 1, 13,
-    3, 0, 2, 2, 1, 3, 3, 2, 0, 1, 3, 0, 2, 1, 11, 3, 0, 2, 10, 1, 3, 2, 11, 0,
-    3, 12, 1, 2, 13, 1, 3, 1, 10, 0, 12, 2, 13, 3, 1, 0, 0, 2, 2, 3, 3, 0, 2, 3,
-    1, 0, 2, 3, 1, 0, 2, 3, 0, 1, 2, 3,
+    0, 1, 3, 0, 2, 1, 10, 11, 13, 1, 2, 0, 3, 12, 20, 13, 10, 30, 11, 2, 1, 30, 20, 0,
+    3, 12, 20, 30, 2, 0, 20, 1, 3, 3, 2, 30, 30, 20, 0, 1, 3, 2, 30, 30, 0, 20, 1, 30,
+    20, 3, 2, 0, 1, 3, 2, 0, 1, 3, 2, 0, 10, 11, 1, 13, 3, 2, 12, 20, 0, 0, 1, 1,
+    3, 3, 2, 2, 0, 1, 3, 2, 0, 1, 3, 2, 1, 0, 3, 2,
 )
 VMEM_LIMIT = 52 * 1024 * 1024
 
@@ -39,18 +43,17 @@
 def step_kernel(dims, res_in, norm_in, win_in, cw_in, cb_in, wx_in, wdt_in, dtb_in, al_in, dsk_in, wo_in, cs_in, ssm_in,
                 res_out, conv_out, ssm_buf,
                 res_ref, norm_ref, win_ref, cw_ref, cb_ref, wx_ref, wdt_ref, dtb_ref, al_ref, dsk_ref, wo_ref, cs_ref,
-                w_buf, send_a, recv_a, send_b, recv_b, send_a2, recv_a2, send_b2, recv_b2, st_send, st_recv, st2_send, st2_recv, stat_t,
-                p_send, p_recv, y_a, y_b, o_send, o_recv, sum_buf, res_buf, dt_buf, dx_buf, bc_buf, yv_buf, xc_buf,
+                w_all, h_send, h_all, sth_send, sth_recv, stz_send, stz_recv, g_send, g_recv, send_a, recv_a, send_b, recv_b, send_a2, recv_a2, send_b2, recv_b2, st_send, st_recv, st2_send, st2_recv, stat_t,
+                p_send, p_recv, y_buf, o_send, o_recv, sum_buf, res_buf, dt_buf, dx_buf, bc_buf, yv_buf, xc_buf,
                 in_sems, *sem_refs):
-    m_a, m_b, m_a2, m_b2, m_st, m_st2, m_p, m_ya, m_yb, m_ya2, m_yb2, m_o, m_s = [(sem_refs[2 * i], sem_refs[2 * i + 1]) for i in range(len(sem_refs) // 2)]
+    m_a, m_b, m_a2, m_b2, m_st, m_st2, m_p, m_y, m_o, m_s, m_w, m_h, m_sth, m_stz, m_g, m_i = [(sem_refs[2 * i], sem_refs[2 * i + 1]) for i in range(len(sem_refs) // 2)]
     n_z, n_y, n_ty, n_str, rows, layers, d_model, n_state, rank, order = dims
     tx, ty = lax.axis_index("tx"), lax.axis_index("ty")
     zi, yi = tx // n_y, tx % n_y
     chans = win_ref.shape[-1]
-    half = chans // 2
-    own_blocks = n_z * n_y // n_ty
-    own_rows = own_blocks * rows
+    cut = chans * CUT // 4
     group = n_y * rows
+    own_rows = group // n_ty
     pk = p_send.shape[1] - rows
     y1, z1, t1 = n_y - 1, n_z - 1, n_ty - 1
     scope = jax.named_scope
@@ -90,19 +93,21 @@
     def split_weight(lyr, part):
         if (lyr, part) not in split:
             split.add((lyr, part))
-            w_buf[lyr, part] = win_ref[lyr, :, part, :]
+            need(("win", lyr))
+            w_all[lyr, part, yi] = win_ref[lyr, :, part, :]
 
     def input_matmul(k, lyr, strm, source, part):
         split_weight(lyr, part)
+        need(("res", strm))
         norm = norm_ref[lyr:lyr + 1, :]
         for zz in range(n_z):
-            res = source[zz * n_y:(zz + 1) * n_y, strm].reshape(group, LANES)
+            res = source[zz, :, strm].reshape(group, LANES)
             if part == 0:
                 st_send[k, zz] = nt_dot(jnp.ones((8, LANES), F32), res * res, lax.Precision.HIGHEST)
-            prod = nn_dot((res * norm).astype(BF16), w_buf[lyr, part]).astype(BF16)
-            send_b[k, part, zz] = prod[:, half:]
+            prod = nn_dot((res * norm).astype(BF16), w_all[lyr, part, yi]).astype(BF16)
+            send_b[k, part, zz] = prod[:, cut:]
             for yy in range(n_y):
-                send_a[k, part, yy, zz * rows:(zz + 1) * rows, :] = prod[yy * rows:(yy + 1) * rows, :half]
+                send_a[k, part, yy, zz * rows:(zz + 1) * rows, :] = prod[yy * rows:(yy + 1) * rows, :cut]
 
     def phase_one(k, part):
         for off in range(1, n_z):
@@ -136,6 +141,11 @@
             send(send_b2.at[k, part, y_peer(off)], recv_b2.at[k, part, off - 1], m_b2, 2 * k + part, at_y(off))
 
     def finish_sum(k, part):
+        if k >= n_str:
+            kh = k - n_str
+            with scope(f"wait_g_{part}"):
+                arrived(g_recv.at[kh, part], m_g, 2 * kh + part)
+            return add_up(g_send[kh, part, zi], [g_recv[kh, part, off - 1] for off in range(1, n_z)])
         with scope(f"wait_2_{part}"):
             arrived(recv_a2.at[k, part], m_a2, 2 * k + part)
             arrived(recv_b2.at[k, part], m_b2, 2 * k + part)
@@ -144,10 +154,47 @@
         return jnp.concatenate([tot_a, tot_b], axis=-1)
 
     def row_scale(k):
-        arrived(st2_recv.at[k], m_st2, k)
-        stat_t[k] = add_up(st2_send[k], [st2_recv[k, off - 1] for off in range(1, n_y)]).T
-        mine = stat_t[k, pl.ds(pl.multiple_of(yi * rows, 8), rows), :][:, :1]
+        if k >= n_str:
+            kh = k - n_str
+            arrived(stz_recv.at[kh], m_stz, kh)
+            total, place = add_up(stz_send[kh], [stz_recv[kh, off - 1] for off in range(1, n_z)]), zi
+        else:
+            arrived(st2_recv.at[k], m_st2, k)
+            total, place = add_up(st2_send[k], [st2_recv[k, off - 1] for off in range(1, n_y)]), yi
+        stat_t[k] = total.T
+        mine = stat_t[k, pl.ds(pl.multiple_of(place * rows, 8), rows), :][:, :1]
         return lax.rsqrt(mine / d_model + NORM_EPS)
+
+    def spread_hidden(k, lyr, strm, source):
+        kh = k - n_str
+        norm = norm_ref[lyr:lyr + 1, :]
+        for yy in range(n_y):
+            res = source[:, yy, strm].reshape(n_z * rows, LANES)
+            sth_send[kh, yy] = nt_dot(jnp.ones((8, LANES), F32), res * res, lax.Precision.HIGHEST)
+            h_send[kh, yy] = (res * norm).astype(BF16)
+        for off in range(1, n_y):
+            send(h_send.at[kh, y_peer(off)], h_all.at[kh, yi], m_h, kh, at_y(off))
+            send(sth_send.at[kh, y_peer(off)], sth_recv.at[kh, off - 1], m_sth, kh, at_y(off))
+        h_all[kh, yi] = h_send[kh, yi]
+
+    def slab_matmul(k, lyr, part):
+        kh = k - n_str
+        if part == 0:
+            with scope(f"wait_h"):
+                arrived(h_all.at[kh, :y1], m_h, kh)
+                arrived(sth_recv.at[kh], m_sth, kh)
+            stz_send[kh] = add_up(sth_send[kh, yi], [sth_recv[kh, off - 1] for off in range(1, n_y)])
+            for off in range(1, n_z):
+                send(stz_send.at[kh], stz_recv.at[kh, off - 1], m_stz, kh, at_z(off))
+        if (lyr, part) not in gathered:
+            gathered.add((lyr, part))
+            with scope(f"wait_i"):
+                arrived(w_all.at[lyr, part, :y1], m_i, 2 * (lyr - 1) + part)
+        hidden = jnp.concatenate([h_all[kh, yy] for yy in range(n_y)], axis=1)
+        prod = nn_dot(hidden, w_all[lyr, part].reshape(n_y * LANES, chans))
+        g_send[kh, part] = prod.astype(BF16).reshape(n_z, rows, chans)
+        for off in range(1, n_z):
+            send(g_send.at[kh, part, z_peer(off)], g_recv.at[kh, part, off - 1], m_g, 2 * kh + part, at_z(off))
 
     def conv_and_proj(k, lyr, mine, x_in):
         taps = [cs_ref[lyr, j, mine, :] for j in range(3)]
@@ -205,9 +252,6 @@
 
         lax.fori_loop(0, rows // 8, update, 0)
 
-    def push(buf, k, zz, yy, sems, slot, device):
-        send(buf.at[k, zz, yy], buf.at[k, zz, yy], sems, slot, device)
-
     def main_thread(strm):
         mine = slice(strm * rows, (strm + 1) * rows)
         source = res_ref
@@ -215,20 +259,23 @@
             k = lyr * n_str + strm
             if lyr:
                 source = gather_sums(k - n_str, lyr - 1, strm, source)
-                with scope(f"matmul_{strm}"):
-                    input_matmul(k, lyr, strm, source, 0)
-            elif strm != order[0]:
-                with scope(f"matmul_{strm}"):
-                    input_matmul(k, lyr, strm, source, 0)
-            sources[k] = source
-            phase_one(k, 0)
-            yield
-            with scope(f"phase2_{strm}"):
-                phase_two(k, 0)
+                with scope(f"hidden_{strm}"):
+                    spread_hidden(k, lyr, strm, source)
+                yield
+                with scope(f"slab_{strm}"):
+                    slab_matmul(k, lyr, 0)
+            else:
+                if strm != lead:
+                    with scope(f"matmul_{strm}"):
+                        input_matmul(k, lyr, strm, source, 0)
+                phase_one(k, 0)
+                yield
+                with scope(f"phase2_{strm}"):
+                    phase_two(k, 0)
             yield
             with scope(f"xconv_{strm}"):
                 scale = row_scale(k)
-                need(7)
+                need("cw", "cb", "cs", "wx")
                 conv_and_proj(k, lyr, mine, (finish_sum(k, 0) * scale).astype(BF16))
             for off in range(1, n_ty):
                 send(p_send.at[k], p_recv.at[k, off - 1], m_p, k, ty_peer(off))
@@ -236,57 +283,37 @@
             with scope(f"wait_p_{strm}"):
                 arrived(p_recv.at[k], m_p, k)
             with scope(f"ssm_{strm}"):
-                need(13 + lyr)
+                need("wdt", "dtb", "al", "dsk", ("ssm", lyr))
                 step_sizes(k, lyr)
                 state_update(k, lyr, strm)
             yield
             with scope(f"gate_{strm}"):
                 z_in = (finish_sum(k, 1) * scale).astype(BF16).astype(F32)
                 gated = ((yv_buf[k] + dsk_ref[lyr:lyr + 1, :] * xc_buf[k].astype(F32)) * (z_in * jax.nn.sigmoid(z_in))).astype(BF16)
-                y_a[k, zi, yi] = gated[:, :half]
-                y_b[k, zi, yi] = gated[:, half:]
+                y_buf[k, yi] = gated
             for off in range(1, n_y):
-                push(y_a, k, zi, yi, m_ya, k * y1 + off - 1, at_y(off))
-            for off in range(1, n_z):
-                push(y_b, k, zi, yi, m_yb, k * z1 + off - 1, at_z(off))
-            for out in range(1, n_z):
-                push(y_a, k, zi, yi, m_ya2, k * z1 + out - 1, at_z(out))
-            for out in range(1, n_y):
-                push(y_b, k, zi, yi, m_yb2, k * n_z, at_y(out))
-            yield
-            with scope(f"fwd_{strm}"):
-                for off in range(1, max(n_y, n_z)):
-                    if off < n_y:
-                        arrived(y_a.at[k, 0, 0], m_ya, k * y1 + off - 1)
-                        for out in range(1, n_z):
-                            push(y_a, k, zi, lax.rem(yi + n_y - off, n_y), m_ya2, k * z1 + out - 1, at_z(out))
-                    if off < n_z:
-                        arrived(y_b.at[k, 0, 0], m_yb, k * z1 + off - 1)
-                        for out in range(1, n_y):
-                            push(y_b, k, lax.rem(zi + n_z - off, n_z), yi, m_yb2, k * n_z + off, at_y(out))
-            yield
-            per_group = n_ty // n_z
-            for off in range(n_z):
-                with scope(f"outmm_{strm}_{off}"):
-                    zz = lax.rem(zi + n_z - off, n_z)
-                    if off:
-                        arrived(y_a.at[k, 0], m_ya2, k * z1 + off - 1)
-                    arrived(y_b.at[k, 0, :y1], m_yb2, k * n_z + off)
-                    part = nn_dot(y_a[k, zz].reshape(group, half), wo_ref[lyr, :half]) + nn_dot(y_b[k, zz].reshape(group, half), wo_ref[lyr, half:])
-                    for i in range(per_group):
-                        o_send[k, zz * per_group + i] = part[i * own_rows:(i + 1) * own_rows].astype(BF16)
-                    for i in range(per_group):
-                        owner = zz * per_group + i
-                        slot = lax.rem(owner - ty + n_ty - 1, n_ty)
-
-                        @pl.when(owner != ty)
-                        def _():
-                            send(o_send.at[k, owner], o_recv.at[k, slot], m_o, k, at_ty(owner))
-
+                send(y_buf.at[k, yi], y_buf.at[k, yi], m_y, k, at_y(off))
+            yield
+            with scope(f"wait_y_{strm}"):
+                arrived(y_buf.at[k, :y1], m_y, k)
+            with scope(f"outmm_{strm}"):
+                if lyr not in gathered:
+                    gathered.add(lyr)
+                    arrived(wo_ref.at[lyr, :z1], m_w, lyr)
+                everyone = y_buf[k].reshape(group, chans)
+                for off in range(n_z):
+                    zz = z_peer(off)
+                    o_send[k, zz] = nn_dot(everyone, wo_ref[lyr, zz]).reshape(n_ty, own_rows, LANES).astype(BF16)
+                    for step in range(n_ty):
+                        owner = lax.rem(ty + step, n_ty)
+                        if off or step:
+                            send(o_send.at[k, zz, owner], o_recv.at[k, zi * n_ty + ty], m_o, k, {"tx": zz * n_y + yi, "ty": owner})
+                o_recv[k, zi * n_ty + ty] = o_send[k, zi, ty]
             yield
             with scope(f"wait_o_{strm}"):
-                arrived(o_recv.at[k], m_o, k)
-            sum_buf[k, ty] = add_up(o_send[k, ty], [o_recv[k, off - 1] for off in range(1, n_ty)]).astype(BF16)
+                arrived(o_recv.at[k, :n_z * n_ty - 1], m_o, k)
+            parts = o_recv[k].astype(F32).reshape(n_z, n_ty, own_rows, LANES)
+            sum_buf[k, ty] = functools.reduce(jnp.add, [parts[:, i] for i in range(n_ty)]).astype(BF16)
             for off in range(1, n_ty):
                 send(sum_buf.at[k, ty], sum_buf.at[k, ty], m_s, k, ty_peer(off))
             yield
@@ -296,61 +323,98 @@
         with scope(f"wait_s_{strm}"):
             arrived(sum_buf.at[k, :t1], m_s, k)
         target = res_out if lyr == layers - 1 else res_buf
-        for blk in range(n_ty):
-            span = slice(blk * own_blocks, (blk + 1) * own_blocks)
-            target[span, strm] = source[span, strm] + sum_buf[k, blk].astype(F32).reshape(own_blocks, rows, LANES)
+        for owner in range(n_ty):
+            blk, low = owner * own_rows // rows, owner * own_rows % rows
+            span = slice(low, low + own_rows)
+            target[:, blk, strm, span, :] = source[:, blk, strm, span, :] + sum_buf[k, owner].astype(F32)
         return target
 
     def gate_thread(strm):
         for lyr in range(layers):
             k = lyr * n_str + strm
+            if lyr:
+                with scope(f"slabz_{strm}"):
+                    slab_matmul(k, lyr, 1)
+                yield
+                continue
             with scope(f"matmulz_{strm}"):
-                input_matmul(k, lyr, strm, sources[k], 1)
+                input_matmul(k, lyr, strm, res_ref, 1)
             phase_one(k, 1)
             yield
             with scope(f"phase2z_{strm}"):
                 phase_two(k, 1)
             yield
 
-    sources = {}
-    moves = [(res_in, res_ref), (norm_in, norm_ref), (win_in, win_ref), (cw_in, cw_ref), (cb_in, cb_ref), (cs_in, cs_ref), (wx_in, wx_ref),
-             (wdt_in, wdt_ref), (dtb_in, dtb_ref), (al_in, al_ref), (dsk_in, dsk_ref), (wo_in, wo_ref)]
-    moves += [(ssm_in.at[lyr], ssm_buf.at[lyr]) for lyr in range(layers)]
-    loads = [pltpu.make_async_copy(src, dst, in_sems.at[i]) for i, (src, dst) in enumerate(moves)]
-    for load in loads[:3]:
-        load.start()
+    def weight_thread():
+        for lyr in range(layers):
+            for piece in range(PIECES):
+                if piece == 0:
+                    need(("wo", lyr))
+                span = pl.ds(piece * width, width)
+                for off in range(1, n_z):
+                    send(wo_ref.at[lyr, zi, span], wo_ref.at[lyr, zi, span], m_w, lyr, at_z(off))
+                yield
+
+    def w_in_thread():
+        for lyr in range(1, layers):
+            for part in range(2):
+                split_weight(lyr, part)
+                for piece in range(PIECES):
+                    span = pl.ds(piece * LANES // PIECES, LANES // PIECES)
+                    for off in range(1, n_y):
+                        send(w_all.at[lyr, part, yi, span], w_all.at[lyr, part, yi, span], m_i, 2 * (lyr - 1) + part, at_y(off))
+                    yield
+
+    gathered = set()
+    width = chans // PIECES
+    lead = next(name for name in order if name < GATE)
+    moves = {("res", lead): (res_in.at[:, :, lead], res_ref.at[:, :, lead]), "norm": (norm_in, norm_ref), ("win", 0): (win_in.at[0], win_ref.at[0])}
+    first = len(moves)
+    moves.update({("res", strm): (res_in.at[:, :, strm], res_ref.at[:, :, strm]) for strm in range(n_str) if strm != lead})
+    moves.update({"cw": (cw_in, cw_ref), "cb": (cb_in, cb_ref), "cs": (cs_in, cs_ref), "wx": (wx_in, wx_ref), "wdt": (wdt_in, wdt_ref)})
+    moves.update({"dtb": (dtb_in, dtb_ref), "al": (al_in, al_ref), "dsk": (dsk_in, dsk_ref)})
+    second = len(moves)
+    moves.update({("wo", lyr): (wo_in.at[lyr], wo_ref.at[lyr, zi]) for lyr in range(layers)})
+    moves.update({("win", lyr): (win_in.at[lyr], win_ref.at[lyr]) for lyr in range(1, layers)})
+    moves.update({("ssm", lyr): (ssm_in.at[lyr], ssm_buf.at[lyr]) for lyr in range(layers)})
+    loads = {name: pltpu.make_async_copy(src, dst, in_sems.at[i]) for i, (name, (src, dst)) in enumerate(moves.items())}
+    for name in list(loads)[:first]:
+        loads[name].start()
+    rest, late = list(loads)[first:second], list(loads)[second:]
+
+    def need(*names):
+        for name in names:
+            if name in loads:
+                loads.pop(name).wait()
 
     barrier = pltpu.get_barrier_semaphore()
-    for off in range(1, n_y):
-        pl.semaphore_signal(barrier, inc=1, device_id=at_y(off), device_id_type=MESH)
-    for off in range(1, n_z):
-        pl.semaphore_signal(barrier, inc=1, device_id=at_z(off), device_id_type=MESH)
-    for off in range(1, n_ty):
-        pl.semaphore_signal(barrier, inc=1, device_id=ty_peer(off), device_id_type=MESH)
-
-    def need(count):
-        while len(moves) - len(loads) < count:
-            loads.pop(0).wait()
-
-    need(3)
-    for load in loads:
-        load.start()
+    peers = [at_y(off) for off in range(1, n_y)] + [at_z(off) for off in range(1, n_z)] + [ty_peer(off) for off in range(1, n_ty)]
+    for peer in peers:
+        pl.semaphore_signal(barrier, inc=1, device_id=peer, device_id_type=MESH)
+    need(("res", lead), "norm", ("win", 0))
+    for name in rest:
+        loads[name].start()
     with scope("matmul_first"):
-        input_matmul(order[0], 0, order[0], res_ref, 0)
+        input_matmul(lead, 0, lead, res_ref, 0)
     with scope("barrier"):
-        pl.semaphore_wait(barrier, n_y + n_z + n_ty - 3)
+        pl.semaphore_wait(barrier, len(peers))
 
     threads = {}
     for strm in range(n_str):
         threads[strm] = main_thread(strm)
         threads[GATE + strm] = gate_thread(strm)
-    for name in order:
+    threads[WEIGHT] = weight_thread()
+    threads[W_IN] = w_in_thread()
+    for turn, name in enumerate(order):
+        if turn == n_str:
+            for load in late:
+                loads[load].start()
         next(threads[name], None)
 
     with scope("drain"):
-        sent = [recv_a, recv_b, recv_a2, recv_b2, st_recv, st2_recv, p_recv, y_a.at[:, 0, :y1], y_b.at[:, 0, :z1],
-                y_a.at[:, :z1], y_b.at[:, :, :y1], o_recv, sum_buf.at[:, :t1]]
-        for ref, sems in zip(sent, [m_a, m_b, m_a2, m_b2, m_st, m_st2, m_p, m_ya, m_yb, m_ya2, m_yb2, m_o, m_s]):
+        sent = [recv_a, recv_b, recv_a2, recv_b2, st_recv, st2_recv, p_recv, y_buf.at[:, :y1], o_recv.at[:, :n_z * n_ty - 1], sum_buf.at[:, :t1], wo_ref.at[:, :z1],
+                h_all.at[:, :y1], sth_recv, stz_recv, g_recv, w_all.at[1:, :, :y1]]
+        for ref, sems in zip(sent, [m_a, m_b, m_a2, m_b2, m_st, m_st2, m_p, m_y, m_o, m_s, m_w, m_h, m_sth, m_stz, m_g, m_i]):
             departed(ref, sems)
 
 
@@ -379,44 +443,54 @@
         rows = batch // n_str
         all_rows, d_local = residual.shape
         rank = w_dt.shape[1]
-        half = chans // 2
-        own = all_rows // n_ty // n_str
+        cut = chans * CUT // 4
+        own = n_y * rows // n_ty
         pk = rows * 2 * n_state // LANES
         ks = layers * n_str
+        kh = ks - n_str
         dims = (n_z, n_y, n_ty, n_str, rows, layers, d_local * n_tx, n_state, rank, order)
         vmem = pl.BlockSpec(memory_space=pltpu.VMEM)
         anyspace = pl.BlockSpec(memory_space=pl.ANY)
         dma = pltpu.SemaphoreType.DMA
-        res_shape = (n_tx, n_str, rows, d_local)
+        res_shape = (n_z, n_y, n_str, rows, d_local)
         conv_shape = (layers, 3, batch, chans)
         ssm_shape = (layers, batch, n_state, chans)
         operands = [
             residual.reshape(res_shape), norm_w, w_in, conv_w.transpose(0, 2, 1), conv_b, w_x.transpose(0, 2, 1), w_dt, dt_bias,
             a_log.transpose(0, 2, 1), d_skip, w_out, conv_state.transpose(0, 3, 1, 2), ssm_state.transpose(0, 1, 3, 2),
         ]
-        scratch = [pltpu.VMEM(op.shape, op.dtype) for op in operands[:-1]]
+        shapes = [op.shape for op in operands[:-1]]
+        shapes[10] = (layers, n_z, chans, d_local)
+        scratch = [pltpu.VMEM(shape, op.dtype) for shape, op in zip(shapes, operands)]
         scratch += [
-            pltpu.VMEM((layers, 2, d_local, chans), BF16),
-            pltpu.VMEM((ks, 2, n_y, n_z * rows, half), BF16),
-            pltpu.VMEM((ks, 2, n_y - 1, n_z * rows, half), BF16),
-            pltpu.VMEM((ks, 2, n_z, n_y * rows, half), BF16),
-            pltpu.VMEM((ks, 2, n_z - 1, n_y * rows, half), BF16),
-            pltpu.VMEM((ks, 2, n_z, rows, half), BF16),
-            pltpu.VMEM((ks, 2, n_z - 1, rows, half), BF16),
-            pltpu.VMEM((ks, 2, n_y, rows, half), BF16),
-            pltpu.VMEM((ks, 2, n_y - 1, rows, half), BF16),
-            pltpu.VMEM((ks, n_z, 8, n_y * rows), F32),
-            pltpu.VMEM((ks, n_z - 1, 8, n_y * rows), F32),
-            pltpu.VMEM((ks, 8, n_y * rows), F32),
-            pltpu.VMEM((ks, n_y - 1, 8, n_y * rows), F32),
+            pltpu.VMEM((layers, 2, n_y, d_local, chans), BF16),
+            pltpu.VMEM((kh, n_y, n_z * rows, d_local), BF16),
+            pltpu.VMEM((kh, n_y, n_z * rows, d_local), BF16),
+            pltpu.VMEM((kh, n_y, 8, n_z * rows), F32),
+            pltpu.VMEM((kh, n_y - 1, 8, n_z * rows), F32),
+            pltpu.VMEM((kh, 8, n_z * rows), F32),
+            pltpu.VMEM((kh, n_z - 1, 8, n_z * rows), F32),
+            pltpu.VMEM((kh, 2, n_z, rows, chans), BF16),
+            pltpu.VMEM((kh, 2, n_z - 1, rows, chans), BF16),
+            pltpu.VMEM((n_str, 2, n_y, n_z * rows, cut), BF16),
+            pltpu.VMEM((n_str, 2, n_y - 1, n_z * rows, cut), BF16),
+            pltpu.VMEM((n_str, 2, n_z, n_y * rows, chans - cut), BF16),
+            pltpu.VMEM((n_str, 2, n_z - 1, n_y * rows, chans - cut), BF16),
+            pltpu.VMEM((n_str, 2, n_z, rows, cut), BF16),
+            pltpu.VMEM((n_str, 2, n_z - 1, rows, cut), BF16),
+            pltpu.VMEM((n_str, 2, n_y, rows, chans - cut), BF16),
+            pltpu.VMEM((n_str, 2, n_y - 1, rows, chans - cut), BF16),
+            pltpu.VMEM((n_str, n_z, 8, n_y * rows), F32),
+            pltpu.VMEM((n_str, n_z - 1, 8, n_y * rows), F32),
+            pltpu.VMEM((n_str, 8, n_y * rows), F32),
+            pltpu.VMEM((n_str, n_y - 1, 8, n_y * rows), F32),
             pltpu.VMEM((ks, n_y * rows, 8), F32),
             pltpu.VMEM((ks, rows + pk, LANES), BF16),
             pltpu.VMEM((ks, n_ty - 1, rows + pk, LANES), BF16),
-            pltpu.VMEM((ks, n_z, n_y, rows, half), BF16),
-            pltpu.VMEM((ks, n_z, n_y, rows, half), BF16),
-            pltpu.VMEM((ks, n_ty, own, d_local), BF16),
-            pltpu.VMEM((ks, n_ty - 1, own, d_local), BF16),
-            pltpu.VMEM((ks, n_ty, own, d_local), BF16),
+            pltpu.VMEM((ks, n_y, rows, chans), BF16),
+            pltpu.VMEM((ks, n_z, n_ty, own, d_local), BF16),
+            pltpu.VMEM((ks, n_z * n_ty, own, d_local), BF16),
+            pltpu.VMEM((ks, n_ty, n_z, own, d_local), BF16),
             pltpu.VMEM(res_shape, F32),
             pltpu.VMEM((ks, rows, chans), F32),
             pltpu.VMEM((ks, rows, chans), F32),
@@ -424,9 +498,8 @@
             pltpu.VMEM((ks, rows, chans), F32),
             pltpu.VMEM((ks, rows, chans), BF16),
         ]
-        y1, z1, t1 = n_y - 1, n_z - 1, n_ty - 1
-        scratch += [dma((len(operands) - 1 + layers,))]
-        for count in [2 * ks, 2 * ks, 2 * ks, 2 * ks, ks, ks, ks, ks * y1, ks * z1, ks * z1, ks * n_z, ks, ks]:
+        scratch += [dma((len(operands) + n_str + 3 * layers,))]
+        for count in [2 * n_str, 2 * n_str, 2 * n_str, 2 * n_str, n_str, n_str, ks, ks, ks, ks, layers, kh, kh, kh, 2 * kh, 2 * (layers - 1)]:
             scratch += [dma, dma((count,))]
         res, conv, ssm = pl.pallas_call(
             functools.partial(step_kernel, dims),

time: 80.7 us -> 73.5 us (0.911)
  Pallas kernels: 79.9 us -> 72.7 us
    pallas_call x1, Pallas kernels: 77.6 us -> 70.4 us  [local_step(): pl.pallas_call(functools.partial(step_kernel, dims), out_shape=(on_chip(r...]
where the time goes in v4:
time: 73.5 us; the launch traced here: 73.3 us
  Pallas kernels  72.7 us (99%)
    pallas_call x1, Pallas kernels, local_step(): pl.pallas_call(functools.partial(step_kernel, dims), out_shape=(on_chip(r...  70.4 us
    pallas_call x1, Pallas kernels, local_step(): pl.pallas_call(store_kernel, out_shape=(jax.ShapeDtypeStruct(res_shape, F...  2.31 us

profile of v4, /device:TPU:1, one launch (start us, length us, event | category | flops | bytes accessed | tf_op | source)
XLA Modules:
  0.0 73.3 jit_solution(1851964329848688880)
XLA Ops:
  0.6 70.4 %shard_map.148 = (f32[4,4,4,16,128]{4,3,2,1,0:T(8,128)S(1)}, bf16[2,3,64,512]{3,2,1,0:T(8,128)(2,1)S(1)}, f32[2,64,16,512]{3,2,1,0:T(8,128)S(1)}) custom-call(f32[4,4,4,16,128]{4,3,2,1,0:T(8,128)} %bitcast.10, f32[2,128]{1,0:T(2,128)} %norm_in.1, bf16[2,128,2,512]{3,2,1,0:T(2,128)(2,1)} %win_in.1, f32[2,4,512]{2,1,0:T(4,128)} %bitcast.14, f32[2,512]{1,0:T(2,128)} %cb_in.1, ...), custom_call_target="tpu_custom_call" | custom-call | tf_op jit(solution)/shard_map/pallas_call | solution.py:504
  71.0 2.3 %shard_map.149 = (f32[4,4,4,16,128]{4,3,2,1,0:T(8,128)}, bf16[2,3,64,512]{3,2,1,0:T(8,128)(2,1)}, f32[2,64,16,512]{3,2,1,0:T(8,128)}) custom-call(f32[4,4,4,16,128]{4,3,2,1,0:T(8,128)S(1)} %get-tuple-element.9.res_ref, bf16[2,3,64,512]{3,2,1,0:T(8,128)(2,1)S(1)} %get-tuple-element.10.conv_ref, f32[2,64,16,512]{3,2,1,0:T(8,128)S(1)} %get-tuple-element.11.ssm_ref), custom_call_target="tpu_custom_call" | custom-call | tf_op jit(solution)/shard_map/pallas_call | solution.py:512

commit v5 on v4

--- a/solution.py
+++ b/solution.py
@@ -20,11 +20,12 @@
 CUT = 2
 STREAMS = 4
 ORDER = (
-    0, 1, 3, 0, 2, 1, 10, 11, 13, 1, 2, 0, 3, 12, 20, 13, 10, 30, 11, 2, 1, 30, 20, 0,
-    3, 12, 20, 30, 2, 0, 20, 1, 3, 3, 2, 30, 30, 20, 0, 1, 3, 2, 30, 30, 0, 20, 1, 30,
-    20, 3, 2, 0, 1, 3, 2, 0, 1, 3, 2, 0, 10, 11, 1, 13, 3, 2, 12, 20, 0, 0, 1, 1,
-    3, 3, 2, 2, 0, 1, 3, 2, 0, 1, 3, 2, 1, 0, 3, 2,
+    1, 2, 11, 3, 1, 0, 20, 30, 2, 1, 3, 11, 13, 20, 0, 10, 3, 12, 1, 30, 13, 30, 2, 20,
+    0, 20, 10, 3, 1, 12, 20, 2, 3, 0, 0, 20, 2, 1, 30, 3, 30, 30, 0, 2, 1, 20, 20, 3,
+    0, 2, 30, 30, 1, 3, 0, 2, 1, 3, 13, 0, 11, 2, 10, 12, 1, 3, 3, 1, 0, 0, 2, 2,
+    3, 1, 0, 2, 3, 1, 0, 2, 1, 0, 3, 2,
 )
+STORES = 1
 VMEM_LIMIT = 52 * 1024 * 1024
 
 
@@ -43,8 +44,8 @@
 def step_kernel(dims, res_in, norm_in, win_in, cw_in, cb_in, wx_in, wdt_in, dtb_in, al_in, dsk_in, wo_in, cs_in, ssm_in,
                 res_out, conv_out, ssm_buf,
                 res_ref, norm_ref, win_ref, cw_ref, cb_ref, wx_ref, wdt_ref, dtb_ref, al_ref, dsk_ref, wo_ref, cs_ref,
-                w_all, h_send, h_all, sth_send, sth_recv, stz_send, stz_recv, g_send, g_recv, send_a, recv_a, send_b, recv_b, send_a2, recv_a2, send_b2, recv_b2, st_send, st_recv, st2_send, st2_recv, stat_t,
-                p_send, p_recv, y_buf, o_send, o_recv, sum_buf, res_buf, dt_buf, dx_buf, bc_buf, yv_buf, xc_buf,
+                w_all, h_send, h_all, sth_send, sth_all, stz_send, stz_recv, g_send, g_recv, send_a, recv_a, send_b, recv_b, send_a2, recv_a2, send_b2, recv_b2, st_send, st_recv, st2_send, st2_recv, stat_t,
+                p_send, p_recv, y_buf, o_send, o_recv, sum_buf, tot_buf, dt_buf, dx_buf, bc_buf, yv_buf, xc_buf,
                 in_sems, *sem_refs):
     m_a, m_b, m_a2, m_b2, m_st, m_st2, m_p, m_y, m_o, m_s, m_w, m_h, m_sth, m_stz, m_g, m_i = [(sem_refs[2 * i], sem_refs[2 * i + 1]) for i in range(len(sem_refs) // 2)]
     n_z, n_y, n_ty, n_str, rows, layers, d_model, n_state, rank, order = dims
@@ -54,6 +55,12 @@
     cut = chans * CUT // 4
     group = n_y * rows
     own_rows = group // n_ty
+    per = n_ty // n_y
+    cy, cc = lax.rem(ty // per + yi, n_y), ty % per
+
+    def chunk_of(owner):
+        return lax.rem(owner // per + yi, n_y) * per + owner % per
+
     pk = p_send.shape[1] - rows
     y1, z1, t1 = n_y - 1, n_z - 1, n_ty - 1
     scope = jax.named_scope
@@ -157,42 +164,68 @@
         if k >= n_str:
             kh = k - n_str
             arrived(stz_recv.at[kh], m_stz, kh)
-            total, place = add_up(stz_send[kh], [stz_recv[kh, off - 1] for off in range(1, n_z)]), zi
+            total = add_up(stz_send[kh], [stz_recv[kh, off - 1] for off in range(1, n_z)])
+            mine = []
+            for c in range(per):
+                stat_t[k, c * n_z * own_rows:(c + 1) * n_z * own_rows, :] = total[c].T
+                mine.append(stat_t[k, pl.ds(pl.multiple_of((c * n_z + zi) * own_rows, own_rows), own_rows), :][:, :1])
+            mine = jnp.concatenate(mine, axis=0)
         else:
             arrived(st2_recv.at[k], m_st2, k)
-            total, place = add_up(st2_send[k], [st2_recv[k, off - 1] for off in range(1, n_y)]), yi
-        stat_t[k] = total.T
-        mine = stat_t[k, pl.ds(pl.multiple_of(place * rows, 8), rows), :][:, :1]
+            stat_t[k, :group] = add_up(st2_send[k], [st2_recv[k, off - 1] for off in range(1, n_y)]).T
+            mine = stat_t[k, pl.ds(pl.multiple_of(yi * rows, 8), rows), :][:, :1]
         return lax.rsqrt(mine / d_model + NORM_EPS)
 
-    def spread_hidden(k, lyr, strm, source):
-        kh = k - n_str
-        norm = norm_ref[lyr:lyr + 1, :]
-        for yy in range(n_y):
-            res = source[:, yy, strm].reshape(n_z * rows, LANES)
-            sth_send[kh, yy] = nt_dot(jnp.ones((8, LANES), F32), res * res, lax.Precision.HIGHEST)
-            h_send[kh, yy] = (res * norm).astype(BF16)
-        for off in range(1, n_y):
-            send(h_send.at[kh, y_peer(off)], h_all.at[kh, yi], m_h, kh, at_y(off))
-            send(sth_send.at[kh, y_peer(off)], sth_recv.at[kh, off - 1], m_sth, kh, at_y(off))
-        h_all[kh, yi] = h_send[kh, yi]
+    def spread_hidden(k, strm, total):
+        tot_buf[strm] = total
+        res = res_ref[:, cy, strm, pl.ds(pl.multiple_of(cc * own_rows, own_rows), own_rows), :] + total
+        norm = norm_ref[k // n_str + 1:k // n_str + 2, :].reshape(1, 1, LANES)
+        sth_send[k] = nt_dot(jnp.ones((8, LANES), F32), (res * res).reshape(n_z * own_rows, LANES), lax.Precision.HIGHEST)
+        h_send[k] = (res * norm).astype(BF16)
+        slot = yi * per + cc
+        for step in range(n_ty):
+            device = {"tx": zi * n_y + cy, "ty": lax.rem(ty + step, n_ty)}
+
+            def deliver():
+                send(h_send.at[k], h_all.at[k, slot], m_h, k, device)
+                send(sth_send.at[k], sth_all.at[k, slot], m_sth, k, device)
+
+            if step:
+                deliver()
+            else:
+                pl.when(cy != yi)(deliver)
+
+        @pl.when(cy == yi)
+        def _():
+            h_all[k, slot] = h_send[k]
+            sth_all[k, slot] = sth_send[k]
 
     def slab_matmul(k, lyr, part):
         kh = k - n_str
         if part == 0:
             with scope(f"wait_h"):
-                arrived(h_all.at[kh, :y1], m_h, kh)
-                arrived(sth_recv.at[kh], m_sth, kh)
-            stz_send[kh] = add_up(sth_send[kh, yi], [sth_recv[kh, off - 1] for off in range(1, n_y)])
+                @pl.when(cy != yi)
+                def _():
+                    arrived(h_all.at[kh], m_h, kh)
+                    arrived(sth_all.at[kh], m_sth, kh)
+
+                @pl.when(cy == yi)
+                def _():
+                    arrived(h_all.at[kh, :n_ty - 1], m_h, kh)
+                    arrived(sth_all.at[kh, :n_ty - 1], m_sth, kh)
+
+            for c in range(per):
+                stz_send[kh, c] = functools.reduce(jnp.add, [sth_all[kh, yy * per + c] for yy in range(n_y)])
             for off in range(1, n_z):
                 send(stz_send.at[kh], stz_recv.at[kh, off - 1], m_stz, kh, at_z(off))
         if (lyr, part) not in gathered:
             gathered.add((lyr, part))
             with scope(f"wait_i"):
                 arrived(w_all.at[lyr, part, :y1], m_i, 2 * (lyr - 1) + part)
-        hidden = jnp.concatenate([h_all[kh, yy] for yy in range(n_y)], axis=1)
-        prod = nn_dot(hidden, w_all[lyr, part].reshape(n_y * LANES, chans))
-        g_send[kh, part] = prod.astype(BF16).reshape(n_z, rows, chans)
+        hidden = jnp.concatenate([h_all[kh, yy * per:(yy + 1) * per].reshape(n_z * rows, LANES) for yy in range(n_y)], axis=1)
+        prod = nn_dot(hidden, w_all[lyr, part].reshape(n_y * LANES, chans)).reshape(per, n_z, own_rows, chans)
+        for zz in range(n_z):
+            g_send[kh, part, zz] = prod[:, zz].reshape(rows, chans).astype(BF16)
         for off in range(1, n_z):
             send(g_send.at[kh, part, z_peer(off)], g_recv.at[kh, part, off - 1], m_g, 2 * kh + part, at_z(off))
 
@@ -254,20 +287,15 @@
 
     def main_thread(strm):
         mine = slice(strm * rows, (strm + 1) * rows)
-        source = res_ref
         for lyr in range(layers):
             k = lyr * n_str + strm
             if lyr:
-                source = gather_sums(k - n_str, lyr - 1, strm, source)
-                with scope(f"hidden_{strm}"):
-                    spread_hidden(k, lyr, strm, source)
-                yield
                 with scope(f"slab_{strm}"):
                     slab_matmul(k, lyr, 0)
             else:
                 if strm != lead:
                     with scope(f"matmul_{strm}"):
-                        input_matmul(k, lyr, strm, source, 0)
+                        input_matmul(k, lyr, strm, res_ref, 0)
                 phase_one(k, 0)
                 yield
                 with scope(f"phase2_{strm}"):
@@ -299,7 +327,7 @@
             with scope(f"outmm_{strm}"):
                 if lyr not in gathered:
                     gathered.add(lyr)
-                    arrived(wo_ref.at[lyr, :z1], m_w, lyr)
+                    arrived(wo_ref.at[lyr, :z1 - 1], m_w, lyr)
                 everyone = y_buf[k].reshape(group, chans)
                 for off in range(n_z):
                     zz = z_peer(off)
@@ -307,27 +335,30 @@
                     for step in range(n_ty):
                         owner = lax.rem(ty + step, n_ty)
                         if off or step:
-                            send(o_send.at[k, zz, owner], o_recv.at[k, zi * n_ty + ty], m_o, k, {"tx": zz * n_y + yi, "ty": owner})
-                o_recv[k, zi * n_ty + ty] = o_send[k, zi, ty]
+                            send(o_send.at[k, zz, chunk_of(owner)], o_recv.at[k, zi * n_ty + ty], m_o, k, {"tx": zz * n_y + yi, "ty": owner})
+                o_recv[k, zi * n_ty + ty] = o_send[k, zi, chunk_of(ty)]
             yield
             with scope(f"wait_o_{strm}"):
                 arrived(o_recv.at[k, :n_z * n_ty - 1], m_o, k)
             parts = o_recv[k].astype(F32).reshape(n_z, n_ty, own_rows, LANES)
-            sum_buf[k, ty] = functools.reduce(jnp.add, [parts[:, i] for i in range(n_ty)]).astype(BF16)
+            total = functools.reduce(jnp.add, [parts[:, i] for i in range(n_ty)])
+            if lyr:
+                total = total + tot_buf[strm]
+            if lyr < layers - 1:
+                with scope(f"hidden_{strm}"):
+                    spread_hidden(k, strm, total)
+                yield
+                continue
+            sum_buf[strm, ty] = total.astype(BF16)
             for off in range(1, n_ty):
-                send(sum_buf.at[k, ty], sum_buf.at[k, ty], m_s, k, ty_peer(off))
-            yield
-        gather_sums(k, lyr, strm, source)
-
-    def gather_sums(k, lyr, strm, source):
+                send(sum_buf.at[strm, ty], sum_buf.at[strm, ty], m_s, strm, ty_peer(off))
+            yield
         with scope(f"wait_s_{strm}"):
-            arrived(sum_buf.at[k, :t1], m_s, k)
-        target = res_out if lyr == layers - 1 else res_buf
+            arrived(sum_buf.at[strm, :t1], m_s, strm)
         for owner in range(n_ty):
-            blk, low = owner * own_rows // rows, owner * own_rows % rows
+            blk, low = lax.rem(owner // per + yi, n_y), owner % per * own_rows
             span = slice(low, low + own_rows)
-            target[:, blk, strm, span, :] = source[:, blk, strm, span, :] + sum_buf[k, owner].astype(F32)
-        return target
+            res_out[:, blk, strm, span, :] = res_ref[:, blk, strm, span, :] + sum_buf[strm, owner].astype(F32)
 
     def gate_thread(strm):
         for lyr in range(layers):
@@ -346,13 +377,26 @@
             yield
 
     def weight_thread():
+        width = chans // 2
+
+        def hand_out(lyr, piece, back, ahead):
+            block = wo_ref.at[lyr, z_peer(n_z - back), pl.ds(piece * width, width)]
+            slot = layers + 2 * lyr + piece if back == 0 and ahead == (1, n_z - 1)[piece] else lyr
+            send(block, block, m_w, slot, at_z(ahead))
+
         for lyr in range(layers):
-            for piece in range(PIECES):
+            for piece in range(2):
                 if piece == 0:
                     need(("wo", lyr))
-                span = pl.ds(piece * width, width)
-                for off in range(1, n_z):
-                    send(wo_ref.at[lyr, zi, span], wo_ref.at[lyr, zi, span], m_w, lyr, at_z(off))
+                hand_out(lyr, piece, 0, 1)
+                if n_z > 2:
+                    hand_out(lyr, piece, 0, n_z - 1)
+                yield
+            for piece in range(2):
+                if n_z > 2:
+                    arrived(wo_ref.at[lyr, 0, pl.ds(piece * width, width)], m_w, layers + 2 * lyr + piece)
+                    ahead = (1, n_z - 1)[piece]
+                    hand_out(lyr, piece, ahead, ahead)
                 yield
 
     def w_in_thread():
@@ -366,7 +410,6 @@
                     yield
 
     gathered = set()
-    width = chans // PIECES
     lead = next(name for name in order if name < GATE)
     moves = {("res", lead): (res_in.at[:, :, lead], res_ref.at[:, :, lead]), "norm": (norm_in, norm_ref), ("win", 0): (win_in.at[0], win_ref.at[0])}
     first = len(moves)
@@ -413,13 +456,29 @@
 
     with scope("drain"):
         sent = [recv_a, recv_b, recv_a2, recv_b2, st_recv, st2_recv, p_recv, y_buf.at[:, :y1], o_recv.at[:, :n_z * n_ty - 1], sum_buf.at[:, :t1], wo_ref.at[:, :z1],
-                h_all.at[:, :y1], sth_recv, stz_recv, g_recv, w_all.at[1:, :, :y1]]
-        for ref, sems in zip(sent, [m_a, m_b, m_a2, m_b2, m_st, m_st2, m_p, m_y, m_o, m_s, m_w, m_h, m_sth, m_stz, m_g, m_i]):
+                stz_recv, g_recv, w_all.at[1:, :, :y1]]
+        for ref, sems in zip(sent, [m_a, m_b, m_a2, m_b2, m_st, m_st2, m_p, m_y, m_o, m_s, m_w, m_stz, m_g, m_i]):
             departed(ref, sems)
 
+        @pl.when(cy != yi)
+        def _():
+            departed(h_all, m_h)
+            departed(sth_all, m_sth)
+
+        @pl.when(cy == yi)
+        def _():
+            departed(h_all.at[:, :n_ty - 1], m_h)
+            departed(sth_all.at[:, :n_ty - 1], m_sth)
+
 
 def store_kernel(res_ref, conv_ref, ssm_ref, res_out, conv_out, ssm_out, sems):
-    copies = [pltpu.make_async_copy(src, dst, sems.at[i]) for i, (src, dst) in enumerate([(ssm_ref, ssm_out), (res_ref, res_out), (conv_ref, conv_out)])]
+    pairs = []
+    step = ssm_ref.shape[1] // STORES
+    for lyr in range(ssm_ref.shape[0]):
+        for i in range(STORES):
+            pairs.append((ssm_ref.at[lyr, i * step:(i + 1) * step], ssm_out.at[lyr, i * step:(i + 1) * step]))
+    pairs += [(res_ref, res_out), (conv_ref, conv_out)]
+    copies = [pltpu.make_async_copy(src, dst, sems.at[i]) for i, (src, dst) in enumerate(pairs)]
     for desc in copies:
         desc.start()
     for desc in copies:
@@ -464,12 +523,12 @@
         scratch = [pltpu.VMEM(shape, op.dtype) for shape, op in zip(shapes, operands)]
         scratch += [
             pltpu.VMEM((layers, 2, n_y, d_local, chans), BF16),
-            pltpu.VMEM((kh, n_y, n_z * rows, d_local), BF16),
-            pltpu.VMEM((kh, n_y, n_z * rows, d_local), BF16),
-            pltpu.VMEM((kh, n_y, 8, n_z * rows), F32),
-            pltpu.VMEM((kh, n_y - 1, 8, n_z * rows), F32),
-            pltpu.VMEM((kh, 8, n_z * rows), F32),
-            pltpu.VMEM((kh, n_z - 1, 8, n_z * rows), F32),
+            pltpu.VMEM((kh, n_z, own, d_local), BF16),
+            pltpu.VMEM((kh, n_ty, n_z, own, d_local), BF16),
+            pltpu.VMEM((kh, 8, n_z * own), F32),
+            pltpu.VMEM((kh, n_ty, 8, n_z * own), F32),
+            pltpu.VMEM((kh, n_ty // n_y, 8, n_z * own), F32),
+            pltpu.VMEM((kh, n_z - 1, n_ty // n_y, 8, n_z * own), F32),
             pltpu.VMEM((kh, 2, n_z, rows, chans), BF16),
             pltpu.VMEM((kh, 2, n_z - 1, rows, chans), BF16),
             pltpu.VMEM((n_str, 2, n_y, n_z * rows, cut), BF16),
@@ -484,14 +543,14 @@
             pltpu.VMEM((n_str, n_z - 1, 8, n_y * rows), F32),
             pltpu.VMEM((n_str, 8, n_y * rows), F32),
             pltpu.VMEM((n_str, n_y - 1, 8, n_y * rows), F32),
-            pltpu.VMEM((ks, n_y * rows, 8), F32),
+            pltpu.VMEM((ks, max(n_y, n_z) * rows, 8), F32),
             pltpu.VMEM((ks, rows + pk, LANES), BF16),
             pltpu.VMEM((ks, n_ty - 1, rows + pk, LANES), BF16),
             pltpu.VMEM((ks, n_y, rows, chans), BF16),
             pltpu.VMEM((ks, n_z, n_ty, own, d_local), BF16),
             pltpu.VMEM((ks, n_z * n_ty, own, d_local), BF16),
-            pltpu.VMEM((ks, n_ty, n_z, own, d_local), BF16),
-            pltpu.VMEM(res_shape, F32),
+            pltpu.VMEM((n_str, n_ty, n_z, own, d_local), BF16),
+            pltpu.VMEM((n_str, n_z, own, d_local), F32),
             pltpu.VMEM((ks, rows, chans), F32),
             pltpu.VMEM((ks, rows, chans), F32),
             pltpu.VMEM((ks, rows, LANES), F32),
@@ -499,7 +558,7 @@
             pltpu.VMEM((ks, rows, chans), BF16),
         ]
         scratch += [dma((len(operands) + n_str + 3 * layers,))]
-        for count in [2 * n_str, 2 * n_str, 2 * n_str, 2 * n_str, n_str, n_str, ks, ks, ks, ks, layers, kh, kh, kh, 2 * kh, 2 * (layers - 1)]:
+        for count in [2 * n_str, 2 * n_str, 2 * n_str, 2 * n_str, n_str, n_str, ks, ks, ks, n_str, 3 * layers, kh, kh, kh, 2 * kh, 2 * (layers - 1)]:
             scratch += [dma, dma((count,))]
         res, conv, ssm = pl.pallas_call(
             functools.partial(step_kernel, dims),
@@ -514,7 +573,7 @@
             out_shape=(jax.ShapeDtypeStruct(res_shape, F32), jax.ShapeDtypeStruct(conv_shape, BF16), jax.ShapeDtypeStruct(ssm_shape, F32)),
             in_specs=[vmem] * 3,
             out_specs=(anyspace,) * 3,
-            scratch_shapes=[dma((3,))],
+            scratch_shapes=[dma((layers * STORES + 2,))],
             compiler_params=pltpu.CompilerParams(vmem_limit_bytes=16 * 1024 * 1024),
         )(*(from_chip(out) for out in (res, conv, ssm)))
         return res.reshape(all_rows, d_local), conv.transpose(0, 2, 3, 1), ssm.transpose(0, 1, 3, 2)

time: 73.5 us -> 71.8 us (0.977)
  Pallas kernels: 72.7 us -> 71 us
    pallas_call x1, Pallas kernels: 70.4 us -> 68.7 us  [local_step(): pl.pallas_call(functools.partial(step_kernel, dims), out_shape=(on_chip(r...]
where the time goes in v5:
time: 71.8 us; the launch traced here: 71.7 us
  Pallas kernels  71 us (99%)
    pallas_call x1, Pallas kernels, local_step(): pl.pallas_call(functools.partial(step_kernel, dims), out_shape=(on_chip(r...  68.7 us
    pallas_call x1, Pallas kernels, local_step(): pl.pallas_call(store_kernel, out_shape=(jax.ShapeDtypeStruct(res_shape, F...  2.32 us

profile of v5, /device:TPU:1, one launch (start us, length us, event | category | flops | bytes accessed | tf_op | source)
XLA Modules:
  0.0 71.7 jit_solution(2683979675133135031)
XLA Ops:
  0.6 68.7 %shard_map.148 = (f32[4,4,4,16,128]{4,3,2,1,0:T(8,128)S(1)}, bf16[2,3,64,512]{3,2,1,0:T(8,128)(2,1)S(1)}, f32[2,64,16,512]{3,2,1,0:T(8,128)S(1)}) custom-call(f32[4,4,4,16,128]{4,3,2,1,0:T(8,128)} %bitcast.10, f32[2,128]{1,0:T(2,128)} %norm_in.1, bf16[2,128,2,512]{3,2,1,0:T(2,128)(2,1)} %win_in.1, f32[2,4,512]{2,1,0:T(4,128)} %bitcast.14, f32[2,512]{1,0:T(2,128)} %cb_in.1, ...), custom_call_target="tpu_custom_call" | custom-call | tf_op jit(solution)/shard_map/pallas_call | solution.py:563
  69.4 2.3 %shard_map.149 = (f32[4,4,4,16,128]{4,3,2,1,0:T(8,128)}, bf16[2,3,64,512]{3,2,1,0:T(8,128)(2,1)}, f32[2,64,16,512]{3,2,1,0:T(8,128)}) custom-call(f32[4,4,4,16,128]{4,3,2,1,0:T(8,128)S(1)} %get-tuple-element.9.res_ref, bf16[2,3,64,512]{3,2,1,0:T(8,128)(2,1)S(1)} %get-tuple-element.10.conv_ref, f32[2,64,16,512]{3,2,1,0:T(8,128)S(1)} %get-tuple-element.11.ssm_ref), custom_call_target="tpu_custom_call" | custom-call | tf_op jit(solution)/shard_map/pallas_call | solution.py:571

commit v6 on v5

--- a/solution.py
+++ b/solution.py
@@ -20,13 +20,17 @@
 CUT = 2
 STREAMS = 4
 ORDER = (
-    1, 2, 11, 3, 1, 0, 20, 30, 2, 1, 3, 11, 13, 20, 0, 10, 3, 12, 1, 30, 13, 30, 2, 20,
-    0, 20, 10, 3, 1, 12, 20, 2, 3, 0, 0, 20, 2, 1, 30, 3, 30, 30, 0, 2, 1, 20, 20, 3,
-    0, 2, 30, 30, 1, 3, 0, 2, 1, 3, 13, 0, 11, 2, 10, 12, 1, 3, 3, 1, 0, 0, 2, 2,
-    3, 1, 0, 2, 3, 1, 0, 2, 1, 0, 3, 2,
+    0, 2, 3, 1, 0, 2, 10, 30, 3, 20, 1, 2, 20, 11, 0, 12, 3, 10, 13, 30, 1, 0, 11, 30,
+    20, 20, 12, 0, 1, 13, 2, 20, 1, 2, 3, 3, 30, 0, 1, 2, 30, 30, 3, 0, 1, 20, 2, 3,
+    30, 30, 0, 1, 2, 3, 0, 20, 1, 20, 10, 2, 11, 3, 12, 13, 0, 1, 0, 1, 2, 2, 3, 3,
+    0, 1, 2, 3, 0, 1, 2, 3, 2, 0, 1, 3,
 )
 STORES = 1
 VMEM_LIMIT = 52 * 1024 * 1024
+
+
+def far(count):
+    return sorted(range(1, count), key=lambda off: -min(off, count - off))
 
 
 def nt_dot(lhs, rhs, precision=None):
@@ -117,10 +121,10 @@
                 send_a[k, part, yy, zz * rows:(zz + 1) * rows, :] = prod[yy * rows:(yy + 1) * rows, :cut]
 
     def phase_one(k, part):
-        for off in range(1, n_z):
+        for off in far(n_z):
             if part == 0:
                 send(st_send.at[k, z_peer(off)], st_recv.at[k, off - 1], m_st, k, at_z(off))
-        for off in range(1, max(n_y, n_z)):
+        for off in far(max(n_y, n_z)):
             if off < n_y:
                 send(send_a.at[k, part, y_peer(off)], recv_a.at[k, part, off - 1], m_a, 2 * k + part, at_y(off))
             if off < n_z:
@@ -130,21 +134,21 @@
         if part == 0:
             arrived(st_recv.at[k], m_st, k)
             st2_send[k] = add_up(st_send[k, zi], [st_recv[k, off - 1] for off in range(1, n_z)])
-            for off in range(1, n_y):
+            for off in far(n_y):
                 send(st2_send.at[k], st2_recv.at[k, off - 1], m_st2, k, at_y(off))
         with scope(f"wait_a1_{part}"):
             arrived(recv_a.at[k, part], m_a, 2 * k + part)
         for zz in range(n_z):
             span = slice(zz * rows, (zz + 1) * rows)
             send_a2[k, part, zz] = add_up(send_a[k, part, yi, span, :], [recv_a[k, part, off - 1, span, :] for off in range(1, n_y)]).astype(BF16)
-        for off in range(1, n_z):
+        for off in far(n_z):
             send(send_a2.at[k, part, z_peer(off)], recv_a2.at[k, part, off - 1], m_a2, 2 * k + part, at_z(off))
         with scope(f"wait_b1_{part}"):
             arrived(recv_b.at[k, part], m_b, 2 * k + part)
         for yy in range(n_y):
             span = slice(yy * rows, (yy + 1) * rows)
             send_b2[k, part, yy] = add_up(send_b[k, part, zi, span, :], [recv_b[k, part, off - 1, span, :] for off in range(1, n_z)]).astype(BF16)
-        for off in range(1, n_y):
+        for off in far(n_y):
             send(send_b2.at[k, part, y_peer(off)], recv_b2.at[k, part, off - 1], m_b2, 2 * k + part, at_y(off))
 
     def finish_sum(k, part):
@@ -183,7 +187,7 @@
         sth_send[k] = nt_dot(jnp.ones((8, LANES), F32), (res * res).reshape(n_z * own_rows, LANES), lax.Precision.HIGHEST)
         h_send[k] = (res * norm).astype(BF16)
         slot = yi * per + cc
-        for step in range(n_ty):
+        for step in far(n_ty) + [0]:
             device = {"tx": zi * n_y + cy, "ty": lax.rem(ty + step, n_ty)}
 
             def deliver():
@@ -216,7 +220,7 @@
 
             for c in range(per):
                 stz_send[kh, c] = functools.reduce(jnp.add, [sth_all[kh, yy * per + c] for yy in range(n_y)])
-            for off in range(1, n_z):
+            for off in far(n_z):
                 send(stz_send.at[kh], stz_recv.at[kh, off - 1], m_stz, kh, at_z(off))
         if (lyr, part) not in gathered:
             gathered.add((lyr, part))
@@ -226,7 +230,7 @@
         prod = nn_dot(hidden, w_all[lyr, part].reshape(n_y * LANES, chans)).reshape(per, n_z, own_rows, chans)
         for zz in range(n_z):
             g_send[kh, part, zz] = prod[:, zz].reshape(rows, chans).astype(BF16)
-        for off in range(1, n_z):
+        for off in far(n_z):
             send(g_send.at[kh, part, z_peer(off)], g_recv.at[kh, part, off - 1], m_g, 2 * kh + part, at_z(off))
 
     def conv_and_proj(k, lyr, mine, x_in):
@@ -305,7 +309,7 @@
                 scale = row_scale(k)
                 need("cw", "cb", "cs", "wx")
                 conv_and_proj(k, lyr, mine, (finish_sum(k, 0) * scale).astype(BF16))
-            for off in range(1, n_ty):
+            for off in far(n_ty):
                 send(p_send.at[k], p_recv.at[k, off - 1], m_p, k, ty_peer(off))
             yield
             with scope(f"wait_p_{strm}"):
@@ -319,7 +323,7 @@
                 z_in = (finish_sum(k, 1) * scale).astype(BF16).astype(F32)
                 gated = ((yv_buf[k] + dsk_ref[lyr:lyr + 1, :] * xc_buf[k].astype(F32)) * (z_in * jax.nn.sigmoid(z_in))).astype(BF16)
                 y_buf[k, yi] = gated
-            for off in range(1, n_y):
+            for off in far(n_y):
                 send(y_buf.at[k, yi], y_buf.at[k, yi], m_y, k, at_y(off))
             yield
             with scope(f"wait_y_{strm}"):
@@ -329,10 +333,10 @@
                     gathered.add(lyr)
                     arrived(wo_ref.at[lyr, :z1 - 1], m_w, lyr)
                 everyone = y_buf[k].reshape(group, chans)
-                for off in range(n_z):
+                for off in far(n_z) + [0]:
                     zz = z_peer(off)
                     o_send[k, zz] = nn_dot(everyone, wo_ref[lyr, zz]).reshape(n_ty, own_rows, LANES).astype(BF16)
-                    for step in range(n_ty):
+                    for step in far(n_ty) + [0]:
                         owner = lax.rem(ty + step, n_ty)
                         if off or step:
                             send(o_send.at[k, zz, chunk_of(owner)], o_recv.at[k, zi * n_ty + ty], m_o, k, {"tx": zz * n_y + yi, "ty": owner})
@@ -350,7 +354,7 @@
                 yield
                 continue
             sum_buf[strm, ty] = total.astype(BF16)
-            for off in range(1, n_ty):
+            for off in far(n_ty):
                 send(sum_buf.at[strm, ty], sum_buf.at[strm, ty], m_s, strm, ty_peer(off))
             yield
         with scope(f"wait_s_{strm}"):
@@ -405,7 +409,7 @@
                 split_weight(lyr, part)
                 for piece in range(PIECES):
                     span = pl.ds(piece * LANES // PIECES, LANES // PIECES)
-                    for off in range(1, n_y):
+                    for off in far(n_y):
                         send(w_all.at[lyr, part, yi, span], w_all.at[lyr, part, yi, span], m_i, 2 * (lyr - 1) + part, at_y(off))
                     yield
 

time: 71.8 us -> 70.6 us (0.983)
  Pallas kernels: 71 us -> 69.8 us
    pallas_call x1, Pallas kernels: 68.7 us -> 67.5 us  [local_step(): pl.pallas_call(functools.partial(step_kernel, dims), out_shape=(on_chip(r...]
where the time goes in v6:
time: 70.6 us; the launch traced here: 70.4 us
  Pallas kernels  69.8 us (99%)
    pallas_call x1, Pallas kernels, local_step(): pl.pallas_call(functools.partial(step_kernel, dims), out_shape=(on_chip(r...  67.5 us
    pallas_call x1, Pallas kernels, local_step(): pl.pallas_call(store_kernel, out_shape=(jax.ShapeDtypeStruct(res_shape, F...  2.32 us

profile of v6, /device:TPU:1, one launch (start us, length us, event | category | flops | bytes accessed | tf_op | source)
XLA Modules:
  0.0 70.4 jit_solution(2136315614325646132)
XLA Ops:
  0.6 67.5 %shard_map.148 = (f32[4,4,4,16,128]{4,3,2,1,0:T(8,128)S(1)}, bf16[2,3,64,512]{3,2,1,0:T(8,128)(2,1)S(1)}, f32[2,64,16,512]{3,2,1,0:T(8,128)S(1)}) custom-call(f32[4,4,4,16,128]{4,3,2,1,0:T(8,128)} %bitcast.10, f32[2,128]{1,0:T(2,128)} %norm_in.1, bf16[2,128,2,512]{3,2,1,0:T(2,128)(2,1)} %win_in.1, f32[2,4,512]{2,1,0:T(4,128)} %bitcast.14, f32[2,512]{1,0:T(2,128)} %cb_in.1, ...), custom_call_target="tpu_custom_call" | custom-call | tf_op jit(solution)/shard_map/pallas_call | solution.py:567
  68.1 2.3 %shard_map.149 = (f32[4,4,4,16,128]{4,3,2,1,0:T(8,128)}, bf16[2,3,64,512]{3,2,1,0:T(8,128)(2,1)}, f32[2,64,16,512]{3,2,1,0:T(8,128)}) custom-call(f32[4,4,4,16,128]{4,3,2,1,0:T(8,128)S(1)} %get-tuple-element.9.res_ref, bf16[2,3,64,512]{3,2,1,0:T(8,128)(2,1)S(1)} %get-tuple-element.10.conv_ref, f32[2,64,16,512]{3,2,1,0:T(8,128)S(1)} %get-tuple-element.11.ssm_ref), custom_call_target="tpu_custom_call" | custom-call | tf_op jit(solution)/shard_map/pallas_call | solution.py:575

commit v7 on v6

--- a/solution.py
+++ b/solution.py
@@ -20,10 +20,10 @@
 CUT = 2
 STREAMS = 4
 ORDER = (
-    0, 2, 3, 1, 0, 2, 10, 30, 3, 20, 1, 2, 20, 11, 0, 12, 3, 10, 13, 30, 1, 0, 11, 30,
-    20, 20, 12, 0, 1, 13, 2, 20, 1, 2, 3, 3, 30, 0, 1, 2, 30, 30, 3, 0, 1, 20, 2, 3,
-    30, 30, 0, 1, 2, 3, 0, 20, 1, 20, 10, 2, 11, 3, 12, 13, 0, 1, 0, 1, 2, 2, 3, 3,
-    0, 1, 2, 3, 0, 1, 2, 3, 2, 0, 1, 3,
+    0, 3, 2, 1, 0, 3, 30, 20, 11, 10, 1, 20, 2, 13, 12, 3, 0, 10, 1, 30, 3, 20, 11, 30,
+    2, 0, 20, 13, 12, 0, 20, 1, 20, 1, 3, 2, 2, 30, 30, 0, 30, 30, 1, 3, 2, 20, 0, 1,
+    3, 2, 30, 0, 1, 3, 2, 0, 20, 10, 1, 11, 3, 13, 2, 12, 0, 0, 1, 1, 3, 3, 2, 2,
+    0, 1, 3, 2, 0, 1, 3, 2, 1, 0, 3, 2,
 )
 STORES = 1
 VMEM_LIMIT = 52 * 1024 * 1024
@@ -49,7 +49,7 @@
                 res_out, conv_out, ssm_buf,
                 res_ref, norm_ref, win_ref, cw_ref, cb_ref, wx_ref, wdt_ref, dtb_ref, al_ref, dsk_ref, wo_ref, cs_ref,
                 w_all, h_send, h_all, sth_send, sth_all, stz_send, stz_recv, g_send, g_recv, send_a, recv_a, send_b, recv_b, send_a2, recv_a2, send_b2, recv_b2, st_send, st_recv, st2_send, st2_recv, stat_t,
-                p_send, p_recv, y_buf, o_send, o_recv, sum_buf, tot_buf, dt_buf, dx_buf, bc_buf, yv_buf, xc_buf,
+                p_send, p_recv, y_buf, o_send, o_recv, sum_buf, tot_buf, neg_buf, dt_buf, dx_buf, bc_buf, yv_buf, xc_buf,
                 in_sems, *sem_refs):
     m_a, m_b, m_a2, m_b2, m_st, m_st2, m_p, m_y, m_o, m_s, m_w, m_h, m_sth, m_stz, m_g, m_i = [(sem_refs[2 * i], sem_refs[2 * i + 1]) for i in range(len(sem_refs) // 2)]
     n_z, n_y, n_ty, n_str, rows, layers, d_model, n_state, rank, order = dims
@@ -184,20 +184,20 @@
         tot_buf[strm] = total
         res = res_ref[:, cy, strm, pl.ds(pl.multiple_of(cc * own_rows, own_rows), own_rows), :] + total
         norm = norm_ref[k // n_str + 1:k // n_str + 2, :].reshape(1, 1, LANES)
-        sth_send[k] = nt_dot(jnp.ones((8, LANES), F32), (res * res).reshape(n_z * own_rows, LANES), lax.Precision.HIGHEST)
         h_send[k] = (res * norm).astype(BF16)
         slot = yi * per + cc
-        for step in far(n_ty) + [0]:
-            device = {"tx": zi * n_y + cy, "ty": lax.rem(ty + step, n_ty)}
-
-            def deliver():
-                send(h_send.at[k], h_all.at[k, slot], m_h, k, device)
-                send(sth_send.at[k], sth_all.at[k, slot], m_sth, k, device)
-
-            if step:
-                deliver()
-            else:
-                pl.when(cy != yi)(deliver)
+
+        def deliver(src, dst, sems):
+            for step in far(n_ty):
+                send(src.at[k], dst.at[k, slot], sems, k, {"tx": zi * n_y + cy, "ty": lax.rem(ty + step, n_ty)})
+
+            @pl.when(cy != yi)
+            def _():
+                send(src.at[k], dst.at[k, slot], sems, k, {"tx": zi * n_y + cy, "ty": ty})
+
+        deliver(h_send, h_all, m_h)
+        sth_send[k] = nt_dot(jnp.ones((8, LANES), F32), (res * res).reshape(n_z * own_rows, LANES), lax.Precision.HIGHEST)
+        deliver(sth_send, sth_all, m_sth)
 
         @pl.when(cy == yi)
         def _():
@@ -270,7 +270,7 @@
         dx_buf[k] = delta * xc_buf[k].astype(F32)
 
     def state_update(k, lyr, strm):
-        neg_a = -jnp.exp(al_ref[lyr])
+        neg_a = neg_buf[lyr]
 
         def update(grp, carry):
             base = pl.multiple_of(grp * 8, 8)
@@ -312,6 +312,10 @@
             for off in far(n_ty):
                 send(p_send.at[k], p_recv.at[k, off - 1], m_p, k, ty_peer(off))
             yield
+            if ("neg", lyr) not in split:
+                split.add(("neg", lyr))
+                need("al")
+                neg_buf[lyr] = -jnp.exp(al_ref[lyr])
             with scope(f"wait_p_{strm}"):
                 arrived(p_recv.at[k], m_p, k)
             with scope(f"ssm_{strm}"):
@@ -555,6 +559,7 @@
             pltpu.VMEM((ks, n_z * n_ty, own, d_local), BF16),
             pltpu.VMEM((n_str, n_ty, n_z, own, d_local), BF16),
             pltpu.VMEM((n_str, n_z, own, d_local), F32),
+            pltpu.VMEM((layers, n_state, chans), F32),
             pltpu.VMEM((ks, rows, chans), F32),
             pltpu.VMEM((ks, rows, chans), F32),
             pltpu.VMEM((ks, rows, LANES), F32),

time: 70.6 us -> 70.5 us (level)
  no operation moved by 1% of the time
where the time goes in v7:
time: 70.5 us; the launch traced here: 70.3 us
  Pallas kernels  69.7 us (99%)
    pallas_call x1, Pallas kernels, local_step(): pl.pallas_call(functools.partial(step_kernel, dims), out_shape=(on_chip(r...  67.4 us
    pallas_call x1, Pallas kernels, local_step(): pl.pallas_call(store_kernel, out_shape=(jax.ShapeDtypeStruct(res_shape, F...  2.32 us

profile of v7, /device:TPU:1, one launch (start us, length us, event | category | flops | bytes accessed | tf_op | source)
XLA Modules:
  0.0 70.3 jit_solution(8384966974992411870)
XLA Ops:
  0.6 67.4 %shard_map.148 = (f32[4,4,4,16,128]{4,3,2,1,0:T(8,128)S(1)}, bf16[2,3,64,512]{3,2,1,0:T(8,128)(2,1)S(1)}, f32[2,64,16,512]{3,2,1,0:T(8,128)S(1)}) custom-call(f32[4,4,4,16,128]{4,3,2,1,0:T(8,128)} %bitcast.10, f32[2,128]{1,0:T(2,128)} %norm_in.1, bf16[2,128,2,512]{3,2,1,0:T(2,128)(2,1)} %win_in.1, f32[2,4,512]{2,1,0:T(4,128)} %bitcast.14, f32[2,512]{1,0:T(2,128)} %cb_in.1, ...), custom_call_target="tpu_custom_call" | custom-call | tf_op jit(solution)/shard_map/pallas_call | solution.py:572
  68.0 2.3 %shard_map.149 = (f32[4,4,4,16,128]{4,3,2,1,0:T(8,128)}, bf16[2,3,64,512]{3,2,1,0:T(8,128)(2,1)}, f32[2,64,16,512]{3,2,1,0:T(8,128)}) custom-call(f32[4,4,4,16,128]{4,3,2,1,0:T(8,128)S(1)} %get-tuple-element.9.res_ref, bf16[2,3,64,512]{3,2,1,0:T(8,128)(2,1)S(1)} %get-tuple-element.10.conv_ref, f32[2,64,16,512]{3,2,1,0:T(8,128)S(1)} %get-tuple-element.11.ssm_ref), custom_call_target="tpu_custom_call" | custom-call | tf_op jit(solution)/shard_map/pallas_call | solution.py:580
